TPU v7x, 256 devices: a 8x8x2 block of a 8x8x16 slice. The times are simulated.
256 devices in a mesh: groups: 2 (over z), section: 64 (over y, x), head: 2 (over core).
Axes of the slice: x: 8, y: 8, z: 2, core: 2. Of those that a mesh axis runs over, the one named last changes fastest.
The devices are a block of a 8x8x16 slice.
Arguments:
- video_tokens: bfloat16 [65536, 1536], P(('groups', 'section', 'head')), parts along dimension 0, may hold values from -6 to 6
- modulation: float32 [6, 1536], P('groups'), parts along dimension 0, may hold values from -3 to 3
- project_weight: bfloat16 [3, 1536, 1536], P(None, None, 'head'), may hold values from -0.15625 to 0.15625
- output_weight: bfloat16 [1536, 1536], P('head'), may hold values from -0.15625 to 0.15625
- norm_gains: float32 [3, 128], replicated, may hold values from 1 to 2
- text_cache: bfloat16 [2, 512, 1536], P(None, 'groups', 'head'), parts along dimension 1, may hold values from -6 to 6
- text_count: int32 [2], P('groups'), parts along dimension 0, may hold values from 1 to 256, as said below
- video_keep: int32 [65536], P('groups'), parts along dimension 0, may hold values 0 or 1
- patch_order: int32 [128], P('groups'), parts along dimension 0, may hold values from 0 to 63, each once
- stale_cache: bfloat16 [2, 65536, 1536], P(None, ('groups', 'section'), 'head'), parts along dimension 1, may hold values from -6 to 6
Outputs:
- updated: bfloat16 [65536, 1536], P(('groups', 'section', 'head')), parts along dimension 0
- fresh_cache: bfloat16 [2, 65536, 1536], P(None, ('groups', 'section'), 'head'), parts along dimension 1
There are 2 independent parts, one for each index of `groups`. A program takes and returns all parts, laid end to end along the dimension named above; an argument that names none is the same for every part. Nothing has to cross between parts.
Inputs may be any that keep to these rules, and one draw needn't show every extreme that they name: The first text_count text tokens are real, the rest are padding. `video_keep`: 1 keeps a video token as a key, 0 marks padding. `patch_order`: each place 0 to 63 is held by exactly one patch.
All inputs are finite; a program needn't handle non-finite values.
Results may differ from a plain program's by a relative error of at most 0.0049.
Values may be sent and summed in bfloat16 or wider, within the bound.
A program may use at most 128 MiB of HBM per device.

v0:
```python
import jax
import jax.numpy as jnp
from jax import lax
from jax.sharding import PartitionSpec as P

epsilon = 1e-06


def copy_for_each(array, axis):
    copies = jnp.broadcast_to(array, (lax.axis_size(axis), *array.shape))
    return lax.all_to_all(copies, axis, split_axis=0, concat_axis=0, tiled=True)


def in_order(pieces, dim):
    dims = list(pieces.shape[1:])
    dims[dim] *= pieces.shape[0]
    return jnp.moveaxis(pieces, 0, dim).reshape(dims)


def gathered_copies(array, axis, dim):
    pieces = copy_for_each(array, axis)
    return in_order(pieces, dim)


def from_behind(array, axis, by):
    count = lax.axis_size(axis)
    pairs = [(i, i + by) for i in range(count) if 0 <= i + by < count]
    return lax.ppermute(array, axis, pairs)


def in_blocks(array, dim, count):
    before, after = (array.shape[:dim], array.shape[dim + 1 :])
    return jnp.moveaxis(array.reshape(*before, count, -1, *after), dim, 0)


def sum_at_owner(array, axis, dim):
    count = lax.axis_size(axis)
    pieces = lax.all_to_all(in_blocks(array, dim, count), axis, 0, 0, tiled=True)
    return jnp.sum(pieces.astype(jnp.float32), axis=0)


def layer_norm(values):
    center = jnp.mean(values, axis=-1, keepdims=True)
    shifted = values - center
    spread = jnp.mean(shifted * shifted, axis=-1, keepdims=True)
    return shifted * lax.rsqrt(spread + epsilon)


def head_norm(inputs, gain_row):
    heads_local = inputs.shape[-1] // gain_row.shape[0]
    per_head = inputs.astype(jnp.float32).reshape(inputs.shape[0], heads_local, gain_row.shape[0])
    scaled = (
        per_head
        * lax.rsqrt(jnp.mean(per_head * per_head, axis=-1, keepdims=True) + epsilon)
        * gain_row
    )
    return scaled.astype(jnp.bfloat16)


def lookup(entries, wanted):
    positions = jnp.arange(entries.shape[0], dtype=jnp.int32)
    return jnp.sum(jnp.where(positions == wanted, entries, 0))


def attend_block(queries, key_rows, values, key_live, score_scale):
    scores = (
        jnp.einsum("qhd,khd->hqk", queries, key_rows, preferred_element_type=jnp.float32)
        * score_scale
    )
    weights = jnp.where(key_live[None, None, :], jnp.exp(scores), 0.0)
    total = jnp.sum(weights, axis=-1)
    numerator = jnp.einsum(
        "hqk,khd->qhd", weights.astype(jnp.bfloat16), values, preferred_element_type=jnp.float32
    )
    return (numerator / jnp.transpose(total)[:, :, None]).astype(jnp.bfloat16)


def on_device(
    video_tokens,
    modulation,
    project_weight,
    output_weight,
    norm_gains,
    text_cache,
    text_count,
    video_keep,
    patch_order,
    stale_cache,
):
    section_count = lax.axis_size("section")
    section_place = lax.axis_index("section")
    head_size = norm_gains.shape[1]
    local_width = project_weight.shape[2]
    local_heads = local_width // head_size
    patch_size = stale_cache.shape[1]
    text_rows = text_cache.shape[1]
    hidden = video_tokens.astype(jnp.float32)
    normed = (layer_norm(hidden) * (1.0 + modulation[1]) + modulation[0]).astype(jnp.bfloat16)
    segment = gathered_copies(normed, "head", 0)
    joined = jnp.einsum("rd,cdh->rch", segment, project_weight, preferred_element_type=jnp.float32)
    projected = joined.reshape(segment.shape[0], 3 * local_width)
    key_raw = projected[:, local_width : 2 * local_width].astype(jnp.bfloat16)
    value_raw = projected[:, 2 * local_width :].astype(jnp.bfloat16)
    fresh_cache = jnp.stack([key_raw, value_raw])
    own_slot = lookup(patch_order, section_place)
    left_place = jnp.maximum(section_place - 1, 0)
    right_place = jnp.minimum(section_place + 1, section_count - 1)
    left_slot = lookup(patch_order, left_place)
    right_slot = lookup(patch_order, right_place)
    to_right = jnp.where(own_slot < right_slot, fresh_cache, stale_cache)
    to_left = jnp.where(own_slot < left_slot, fresh_cache, stale_cache)
    left_cache = from_behind(to_right, "section", 1)
    right_cache = from_behind(to_left, "section", -1)
    keep_left = lax.dynamic_slice_in_dim(video_keep, left_place * patch_size, patch_size) > 0
    keep_own = lax.dynamic_slice_in_dim(video_keep, section_place * patch_size, patch_size) > 0
    keep_right = lax.dynamic_slice_in_dim(video_keep, right_place * patch_size, patch_size) > 0
    text_live = jnp.arange(text_rows, dtype=jnp.int32) < text_count[0]
    key_live = jnp.concatenate(
        [
            keep_left & (section_place > 0),
            keep_own,
            keep_right & (section_place < section_count - 1),
            text_live,
        ]
    )
    video_keys = head_norm(
        jnp.concatenate([left_cache[0], key_raw, right_cache[0]], axis=0), norm_gains[1]
    )
    text_keys = head_norm(text_cache[0], norm_gains[2])
    all_keys = jnp.concatenate([video_keys, text_keys], axis=0)
    values = jnp.concatenate(
        [left_cache[1], value_raw, right_cache[1], text_cache[1]], axis=0
    ).reshape(-1, local_heads, head_size)
    queries = head_norm(projected[:, :local_width], norm_gains[0])
    block_rows = min(patch_size, 512)
    score_scale = head_size ** (-0.5)

    def attend(query_block):
        return attend_block(query_block, all_keys, values, key_live, score_scale)

    attended = lax.map(
        attend, queries.reshape(patch_size // block_rows, block_rows, local_heads, head_size)
    ).reshape(patch_size, local_width)
    mixed_rows = sum_at_owner(
        jnp.dot(attended, output_weight, preferred_element_type=jnp.float32).astype(jnp.bfloat16),
        "head",
        0,
    )
    updated = (hidden + modulation[2] * mixed_rows).astype(jnp.bfloat16)
    return (updated, fresh_cache)


def solution(mesh):
    placed = (
        P(("groups", "section", "head"), None),
        P("groups", None),
        P(None, None, "head"),
        P("head", None),
        P(),
        P(None, "groups", "head"),
        P("groups"),
        P("groups"),
        P("groups"),
        P(None, ("groups", "section"), "head"),
    )
    return jax.shard_map(
        on_device,
        mesh=mesh,
        in_specs=placed,
        out_specs=(P(("groups", "section", "head"), None), P(None, ("groups", "section"), "head")),
        check_vma=False,
    )
```

profile of v0, /device:TPU:513, one launch (start us, length us, event | category | flops | bytes accessed | tf_op | source)
XLA Modules:
  0.0 151.1 jit_solution(6374956476702802500)
XLA Ops:
  0.6 0.0 copy-start
  0.6 1.5 convert_reduce_fusion.1
  2.1 1.5 fusion.23
  3.6 0.9 slice_reduce_fusion.1
  4.5 1.5 fusion.26
  6.0 0.0 copy-start.13
  6.0 1.2 broadcast_in_dim.40
  7.3 25.0 %all-to-all-start = ((bf16[2,256,1536]{2,1,0:T(8,128)(2,1)}), bf16[2,256,1536]{2,1,0:T(8,128)(2,1)}, u32[]{:S(2)}, u32[]{:S(2)}) async-start(bf16[2,256,1536]{2,1,0:T(8,128)(2,1)} %broadcast_in_dim.40), calls=%async_computation | async-start | bytes 3145728 | tf_op jit(solution)/shard_map/all_to_all | solution.py:11
  32.3 0.7 fusion.38
  35.6 10.3 %copy.20 = bf16[3,1536,768]{1,2,0:T(8,128)(2,1)} copy(bf16[3,1536,768]{2,1,0:T(8,128)(2,1)} %param.12) | data formatting | bytes 14155776 | tf_op args[2]
  45.9 0.0 all-to-all-done
  45.9 9.6 %fusion.48 = (bf16[512,2304]{1,0:T(8,128)(2,1)S(1)}, f32[512,2304]{1,0:T(8,128)}) fusion(bf16[512,1536]{1,0:T(8,128)(2,1)} %bitcast, bf16[2304,1536]{1,0:T(8,128)(2,1)} %bitcast.37), kind=kOutput, calls=%fused_computation.81 | convolution fusion | flops 3625058304 | bytes 15728640 | tf_op jit(solution)/shard_map/rd,cdh->rch/dot_general | solution.py:100
  55.5 1.1 fusion.44
  56.6 0.6 copy-done.4
  57.2 1.4 broadcast_select_fusion.1
  58.5 1.5 broadcast_select_fusion
  60.1 0.1 copy-done.5
  60.2 1.3 collective-permute-start.1
  61.5 5.2 %collective-permute-start = (bf16[2,512,768]{2,1,0:T(8,128)(2,1)}, bf16[2,512,768]{2,1,0:T(8,128)(2,1)}, u32[]{:S(2)}, u32[]{:S(2)}) collective-permute-start(bf16[2,512,768]{2,1,0:T(8,128)(2,1)} %get-tuple-element.26), channel_id=1, source_target_pairs={{0,2},{2,4},{4,6},{6,8},{8,10},{10,12},{12,14},{14,16},{16,18},{18... | collective-permute-start | bytes 4718600 | tf_op jit(solution)/shard_map/ppermute | solution.py:28
  67.3 0.5 iota_compare_fusion
  67.8 0.9 fusion.35
  68.7 1.9 %fusion.47 = (bf16[1,256,768]{2,1,0:T(8,128)(2,1)S(1)}, bf16[1,256,768]{2,1,0:T(8,128)(2,1)}) fusion(bf16[2,256,768]{2,1,0:T(8,128)(2,1)} %param.15), kind=kLoop, calls=%fused_computation.80 | loop fusion | bytes 1572864 | tf_op jit(solution)/shard_map/slice | solution.py:132
  70.6 0.6 pad_add_fusion
  71.2 0.9 copy.24
  72.1 1.2 copy.36
  73.3 1.1 copy.33
  74.3 2.3 %copy.22 = bf16[512,768]{0,1:T(8,128)(2,1)} copy(bf16[512,768]{1,0:T(8,128)(2,1)} %get-tuple-element.28) | data formatting | bytes 1572864 | tf_op jit(solution)/shard_map/slice | solution.py:103
  76.6 1.2 copy.27
  77.8 1.5 copy.30
  79.3 2.7 %slice.66 = f32[512,768]{1,0:T(8,128)} slice(f32[512,2304]{1,0:T(8,128)} %get-tuple-element.45), slice={[0:512], [0:768]} | slice | bytes 3145728 | tf_op jit(solution)/shard_map/slice | solution.py:134
  82.0 3.0 %copy.25 = f32[512,768]{0,1:T(8,128)} copy(f32[512,768]{1,0:T(8,128)} %slice.66) | data formatting | bytes 3145728 | tf_op jit(solution)/shard_map/slice | solution.py:134
  85.0 0.1 multiply_reduce_fusion.1
  85.1 1.7 %multiply_reduce_fusion = f32[512,6]{0,1:T(8,128)S(1)} fusion(f32[512,6,128]{0,2,1:T(8,128)} %bitcast.38), kind=kLoop, calls=%fused_computation.40 | loop fusion | flops 783360 | bytes 1585152 | tf_op jit(solution)/shard_map/reduce_sum | solution.py:54
  86.8 1.3 slice_bitcast_fusion.2
  88.1 0.6 add_rsqrt_fusion.1
  88.7 0.3 multiply_convert_fusion.2
  89.0 9.3 %collective-permute-done.1 = bf16[2,512,768]{2,1,0:T(8,128)(2,1)} collective-permute-done((bf16[2,512,768]{2,1,0:T(8,128)(2,1)}, bf16[2,512,768]{2,1,0:T(8,128)(2,1)}, u32[]{:S(2)}, u32[]{:S(2)}) %collective-permute-start.1) | collective-permute-done | bytes 1572896 | tf_op jit(solution)/shard_map/ppermute | solution.py:28
  98.3 2.6 %fusion.46 = (bf16[1,512,768]{2,1,0:T(8,128)(2,1)}, bf16[1,512,768]{2,1,0:T(8,128)(2,1)}) fusion(bf16[2,512,768]{2,1,0:T(8,128)(2,1)} %collective-permute-done.1), kind=kLoop, calls=%fused_computation.79 | loop fusion | bytes 3145728 | tf_op jit(solution)/shard_map/slice | solution.py:132
  101.0 2.3 %copy.23 = bf16[1,512,768]{1,2,0:T(8,128)(2,1)} copy(bf16[1,512,768]{2,1,0:T(8,128)(2,1)} %get-tuple-element.34) | data formatting | bytes 1572864 | tf_op jit(solution)/shard_map/slice | solution.py:132
  103.3 2.3 %copy.28 = bf16[1,512,768]{1,2,0:T(8,128)(2,1)} copy(bf16[1,512,768]{2,1,0:T(8,128)(2,1)} %get-tuple-element.35) | data formatting | bytes 1572864 | tf_op jit(solution)/shard_map/slice | solution.py:127
  105.6 2.3 %copy.31 = bf16[512,6,128]{2,0,1:T(8,128)(2,1)} copy(bf16[512,6,128]{0,2,1:T(8,128)(2,1)} %bitcast.44) | data formatting | bytes 1572864 | tf_op jit(solution)/shard_map/concatenate | solution.py:127
  107.9 0.0 collective-permute-done
  107.9 2.6 %fusion.45 = (bf16[1,512,768]{2,1,0:T(8,128)(2,1)}, bf16[1,512,768]{2,1,0:T(8,128)(2,1)}) fusion(bf16[2,512,768]{2,1,0:T(8,128)(2,1)} %collective-permute-done), kind=kLoop, calls=%fused_computation.78 | loop fusion | bytes 3145728 | tf_op jit(solution)/shard_map/slice | solution.py:132
  110.5 2.3 %copy.21 = bf16[1,512,768]{1,2,0:T(8,128)(2,1)} copy(bf16[1,512,768]{2,1,0:T(8,128)(2,1)} %get-tuple-element.32) | data formatting | bytes 1572864 | tf_op jit(solution)/shard_map/slice | solution.py:132
  112.8 2.3 %copy.26 = bf16[1,512,768]{1,2,0:T(8,128)(2,1)} copy(bf16[1,512,768]{2,1,0:T(8,128)(2,1)} %get-tuple-element.33) | data formatting | bytes 1572864 | tf_op jit(solution)/shard_map/slice | solution.py:127
  115.1 2.3 %copy.29 = bf16[512,6,128]{2,0,1:T(8,128)(2,1)} copy(bf16[512,6,128]{0,2,1:T(8,128)(2,1)} %bitcast.45) | data formatting | bytes 1572864 | tf_op jit(solution)/shard_map/concatenate | solution.py:127
  117.4 2.8 %fusion.7 = f32[1536,6]{0,1:T(8,128)S(1)} fusion(bf16[512,6,128]{2,0,1:T(8,128)(2,1)} %copy.31, bf16[512,6,128]{2,0,1:T(8,128)(2,1)S(1)} %copy.30, bf16[512,6,128]{2,0,1:T(8,128)(2,1)} %copy.29), kind=kLoop, calls=%fused_computation.9 | loop fusion | flops 9427968 | bytes 2396160 | tf_op jit(solution)/shard_map/reduce_sum | solution.py:54
  120.2 0.0 copy-done.2
  120.2 0.0 copy-done.3
  120.2 0.0 copy-start.6
  120.2 0.0 copy-start.12
  120.2 0.0 copy-start.14
  120.2 1.7 %fusion.9 = bf16[1536,6,128]{2,0,1:T(8,128)(2,1)S(1)} fusion(f32[128]{0:T(128)S(1)} %get-tuple-element.43, f32[1536,6]{0,1:T(8,128)S(1)} %add_rsqrt_fusion, bf16[512,6,128]{2,0,1:T(8,128)(2,1)S(1)} %copy-done.2, bf16[512,6,128]{2,0,1:T(8,128)(2,1)S(1)} %copy.30, bf16[512,6,128]{2,0,1:T(8,128)(2,1)S(1)} %copy-done.3), kind=kLoop, calls=%fused_computation.11 | loop fusion | flops 10616832 | bytes 4755968 | tf_op jit(solution)/shard_map/convert_element_type | solution.py:57
  121.9 0.0 copy-done.6
  121.9 0.0 copy-done.12
  121.9 0.0 copy-done.14
  121.9 0.0 copy-start.8
  122.0 10.0 %fusion = (f32[6,512]{1,0:T(8,128)S(1)}, f32[6,512,1792]{2,1,0:T(8,128)}) fusion(pred[1792]{0:T(1024)(128)(4,1)S(1)} %pad_add_fusion, bf16[256,6,128]{2,0,1:T(8,128)(2,1)S(1)} %multiply_convert_fusion.2, bf16[1536,6,128]{2,0,1:T(8,128)(2,1)S(1)} %fusion.9, f32[512,6,128]{0,2,1:T(8,128)S(1)} %bitcast.39, f32[128]{0:T(128)S(1)} %copy-done.14, ...), kind=kOutput, calls=%fused_computation.1 | convolution fusion | flops 1432482816 | bytes 26372352 | tf_op jit(solution)/shard_map/while/body/eval_jaxpr/qhd,khd->hqk/dot_general | solution.py:67
  131.9 9.9 %fusion.28 = bf16[512,6,128]{0,2,1:T(8,128)(2,1)S(1)} fusion(f32[6,512,1792]{2,1,0:T(8,128)} %get-tuple-element.47, pred[1792]{0:T(1024)(128)(4,1)S(1)} %pad_add_fusion, bf16[256,6,128]{0,2,1:T(8,128)(2,1)S(1)} %bitcast.50, bf16[512,6,128]{0,2,1:T(8,128)(2,1)S(1)} %bitcast.48, bf16[512,6,128]{0,2,1:T(8,128)(2,1)S(1)} %bitcast.47, ...), kind=kOutput, calls=%fused_computation.38 | convolution fusion | flops 1437597696 | bytes 25573120 | tf_op jit(solution)/shard_map/while/body/eval_jaxpr/hqk,khd->qhd/dot_general | solution.py:72
  141.9 1.4 convolution_convert_fusion
  143.3 5.5 %all_to_all.10 = bf16[2,256,1536]{2,1,0:T(8,128)(2,1)S(1)} all-to-all(bf16[2,256,1536]{2,1,0:T(8,128)(2,1)S(1)} %bitcast.40), channel_id=1, replica_groups=mesh['groups'=2,'section'=64,'head'=2] {'head'}, dimensions={0} | all-to-all | bytes 3145728 | tf_op jit(solution)/shard_map/all_to_all | solution.py:38
  148.8 0.2 convert_reduce_fusion
  149.1 0.9 copy-done.1
  150.0 1.1 fusion.27
  (20 shorter events, 0.1 us)
Async XLA Ops:
  0.6 141.2 %copy-start = (bf16[768,1536]{1,0:T(8,128)(2,1)S(1)}, bf16[768,1536]{1,0:T(8,128)(2,1)}, u32[]{:S(2)}) copy-start(bf16[768,1536]{1,0:T(8,128)(2,1)} %param.13) | copy-start | bytes 7077892
  6.0 26.3 %copy-start.13 = (s32[64]{0:T(128)S(1)}, s32[64]{0:T(128)}, u32[]{:S(2)}) copy-start(s32[64]{0:T(128)} %param.18) | copy-start | bytes 772
  7.3 38.6 %all-to-all-start = ((bf16[2,256,1536]{2,1,0:T(8,128)(2,1)}), bf16[2,256,1536]{2,1,0:T(8,128)(2,1)}, u32[]{:S(2)}, u32[]{:S(2)}) async-start(bf16[2,256,1536]{2,1,0:T(8,128)(2,1)} %broadcast_in_dim.40), calls=%async_computation | async-start | bytes 3145728 | tf_op jit(solution)/shard_map/all_to_all | solution.py:11
  55.5 1.7 %copy-start.4 = (bf16[2,512,768]{2,1,0:T(8,128)(2,1)S(1)}, bf16[2,512,768]{2,1,0:T(8,128)(2,1)}, u32[]{:S(2)}) copy-start(bf16[2,512,768]{2,1,0:T(8,128)(2,1)} %param.19) | copy-start | bytes 4718596
  58.5 1.7 %copy-start.5 = (bf16[2,512,768]{2,1,0:T(8,128)(2,1)}, bf16[2,512,768]{2,1,0:T(8,128)(2,1)S(1)}, u32[]{:S(2)}) copy-start(bf16[2,512,768]{2,1,0:T(8,128)(2,1)S(1)} %get-tuple-element.27) | copy-start | bytes 4718596
  60.2 38.1 %collective-permute-start.1 = (bf16[2,512,768]{2,1,0:T(8,128)(2,1)}, bf16[2,512,768]{2,1,0:T(8,128)(2,1)}, u32[]{:S(2)}, u32[]{:S(2)}) collective-permute-start(bf16[2,512,768]{2,1,0:T(8,128)(2,1)} %broadcast_select_fusion), channel_id=1, source_target_pairs={{2,0},{4,2},{6,4},{8,6},{10,8},{12,10},{14,12},{16,14},{18,16},{20... | collective-permute-start | bytes 4718600 | tf_op jit(solution)/shard_map/ppermute | solution.py:28
  61.5 46.4 %collective-permute-start = (bf16[2,512,768]{2,1,0:T(8,128)(2,1)}, bf16[2,512,768]{2,1,0:T(8,128)(2,1)}, u32[]{:S(2)}, u32[]{:S(2)}) collective-permute-start(bf16[2,512,768]{2,1,0:T(8,128)(2,1)} %get-tuple-element.26), channel_id=1, source_target_pairs={{0,2},{2,4},{4,6},{6,8},{8,10},{10,12},{12,14},{14,16},{16,18},{18... | collective-permute-start | bytes 4718600 | tf_op jit(solution)/shard_map/ppermute | solution.py:28
  85.0 3.7 %copy-start.7 = (f32[256,6,128]{2,0,1:T(8,128)S(1)}, f32[256,6,128]{2,0,1:T(8,128)}, u32[]{:S(2)}) copy-start(f32[256,6,128]{2,0,1:T(8,128)} %copy.33) | copy-start | bytes 2359300
  117.4 2.8 %copy-start.2 = (bf16[512,6,128]{2,0,1:T(8,128)(2,1)S(1)}, bf16[512,6,128]{2,0,1:T(8,128)(2,1)}, u32[]{:S(2)}) copy-start(bf16[512,6,128]{2,0,1:T(8,128)(2,1)} %copy.31) | copy-start | bytes 2359300
  117.4 2.8 %copy-start.3 = (bf16[512,6,128]{2,0,1:T(8,128)(2,1)S(1)}, bf16[512,6,128]{2,0,1:T(8,128)(2,1)}, u32[]{:S(2)}) copy-start(bf16[512,6,128]{2,0,1:T(8,128)(2,1)} %copy.29) | copy-start | bytes 2359300
  120.2 1.7 %copy-start.6 = (f32[512,768]{0,1:T(8,128)S(1)}, f32[512,768]{0,1:T(8,128)}, u32[]{:S(2)}) copy-start(f32[512,768]{0,1:T(8,128)} %copy.25) | copy-start | bytes 4718596
  120.2 1.7 %copy-start.12 = (f32[512,6]{0,1:T(8,128)S(1)}, f32[512,6]{0,1:T(8,128)}, u32[]{:S(2)}) copy-start(f32[512,6]{0,1:T(8,128)} %add_rsqrt_fusion.1) | copy-start | bytes 36868
  120.2 1.7 %copy-start.14 = (f32[128]{0:T(128)S(1)}, f32[128]{0:T(128)}, u32[]{:S(2)}) copy-start(f32[128]{0:T(128)} %get-tuple-element.41) | copy-start | bytes 1540
  121.9 10.0 %copy-start.8 = (bf16[512,768]{0,1:T(8,128)(2,1)S(1)}, bf16[512,768]{0,1:T(8,128)(2,1)}, u32[]{:S(2)}) copy-start(bf16[512,768]{0,1:T(8,128)(2,1)} %copy.22) | copy-start | bytes 2359300
  121.9 10.0 %copy-start.9 = (bf16[1,512,768]{1,2,0:T(8,128)(2,1)S(1)}, bf16[1,512,768]{1,2,0:T(8,128)(2,1)}, u32[]{:S(2)}) copy-start(bf16[1,512,768]{1,2,0:T(8,128)(2,1)} %copy.23) | copy-start | bytes 2359300
  121.9 10.0 %copy-start.10 = (bf16[1,512,768]{1,2,0:T(8,128)(2,1)S(1)}, bf16[1,512,768]{1,2,0:T(8,128)(2,1)}, u32[]{:S(2)}) copy-start(bf16[1,512,768]{1,2,0:T(8,128)(2,1)} %copy.21) | copy-start | bytes 2359300
  121.9 10.0 %copy-start.11 = (bf16[1,256,768]{1,2,0:T(8,128)(2,1)S(1)}, bf16[1,256,768]{1,2,0:T(8,128)(2,1)}, u32[]{:S(2)}) copy-start(bf16[1,256,768]{1,2,0:T(8,128)(2,1)} %copy.24) | copy-start | bytes 1179652
  148.8 1.1 copy-start.1
where the time goes:
time: 152 us; the launch traced here: 151 us
  local copies, waits for them, and re-layouts  50.4 us (33%)
  starting transfers between devices  31.5 us (21%)
  matrix products  30.9 us (20%)
  other arithmetic  19.3 us (13%)
  waiting for transfers between devices  9.35 us (6%)
  blocking collectives  5.55 us (4%)
  between operations  4.12 us (3%)
    all_to_all x1, starting transfers between devices, copy_for_each(): return lax.all_to_all(copies, axis, split_axis=0, concat_axis=0, tiled=True)  25 us
    unnamed x32, local copies, waits for them, and re-layouts  13.1 us
    dot_general x1, matrix products, attend_block(): jnp.einsum('qhd,khd->hqk', queries, key_rows, preferred_element_type=jnp....  9.97 us
    dot_general x1, matrix products, attend_block(): jnp.einsum('hqk,khd->qhd', weights.astype(jnp.bfloat16), values, preferre...  9.9 us
    dot_general x1, matrix products, on_device(): jnp.einsum('rd,cdh->rch', segment, project_weight, preferred_element_type...  9.58 us
    ppermute x2, waiting for transfers between devices, from_behind(): return lax.ppermute(array, axis, pairs)  9.35 us
    ppermute x2, starting transfers between devices, from_behind(): return lax.ppermute(array, axis, pairs)  6.48 us
    concatenate x3, local copies, waits for them, and re-layouts, on_device(): jnp.concatenate([left_cache[0], key_raw, right_cache[0]], axis=0)  6.08 us
  transfers between devices with their start and end apart: 3, of which 1 were waited for; matrix products, arithmetic and copies ran while one was open for 28% of the time, Pallas kernels for 0%

commit v1 on v0

v1 whole, which is shorter than its diff:
```python
import functools
import math

import jax
import jax.numpy as jnp
from jax import lax
from jax.experimental import pallas as pl
from jax.experimental.pallas import tpu as pltpu
from jax.sharding import PartitionSpec as P

epsilon = 1e-06
CHUNKS = 4
F32 = jnp.float32
BF16 = jnp.bfloat16
MESH = pl.DeviceIdType.MESH
NT = (((1,), (1,)), ((), ()))


def matmul(a, b):
    return jnp.dot(a, b, preferred_element_type=F32)


def head_norm(values, gain):
    square = jnp.mean(values * values, axis=-1, keepdims=True)
    return values * lax.rsqrt(square + epsilon) * gain


def kernel(
    order_s, count_s, x_h, mod_h, w_h, wo_h, gains_h, text_h, keep_h, stale_h,
    updated_h, fresh_h,
    x_v, mod_v, w_v, wo_v, gains_v, text_v, keep_v, stale_v,
    normed, message, arrived, fresh_v, q_own, kbuf, vbuf, mbuf, kst, vst, nq, acc,
    r_out, r_in, t_out, t_in, attended, y_out, y_in, upd_v,
    load_sem, part_send, part_recv, p1_send, p1_recv, f_send, f_recv,
    r_send, r_recv, t_send, t_recv, y_send, y_recv, out_sem, fresh_sem,
):
    rows, width = x_v.shape
    patch, local = stale_v.shape[1], stale_v.shape[2]
    text_rows = text_v.shape[1]
    hd = gains_v.shape[1]
    heads = local // hd
    half_heads = heads // 2
    half = half_heads * hd
    sub = rows // CHUNKS
    keys = 4 * sub
    own_chunks = patch // keys
    sections = lax.axis_size("section")
    place = lax.axis_index("section")
    h = lax.axis_index("head")
    right = lax.rem(place + 1, sections)
    left = lax.rem(place + sections - 1, sections)
    nbr_of = ({"section": left}, {"section": right})
    partner = {"head": 1 - h}

    loads = [
        pltpu.make_async_copy(src, dst, load_sem.at[i])
        for i, (src, dst) in enumerate(
            [
                (x_h, x_v), (mod_h, mod_v), (stale_h, stale_v), (gains_h, gains_v), (keep_h, keep_v),
                (text_h, text_v), (w_h, w_v), (wo_h, wo_v),
            ]
        )
    ]
    for load in loads:
        load.start()

    barrier = pltpu.get_barrier_semaphore()
    for device in (nbr_of[0], nbr_of[1], partner):
        pl.semaphore_signal(barrier, inc=1, device_id=device, device_id_type=MESH)

    own_slot = order_s[place]
    slot = (order_s[left], order_s[right])
    exists = (place > 0, place < sections - 1)
    one = jnp.int32(1)
    zero = jnp.int32(0)
    is_b = [jnp.where(slot[n] < own_slot, one, zero) * jnp.where(exists[n], one, zero) for n in range(2)]
    is_a = [jnp.where(slot[n] > own_slot, one, zero) * jnp.where(exists[n], one, zero) for n in range(2)]
    gives = [jnp.where(own_slot < slot[n], one, zero) for n in range(2)]

    def full(flag, shape):
        return jnp.full(shape, flag, jnp.int32) > 0

    for i in (0, 1, 2):
        loads[i].wait()
    scale = 1.0 + mod_v[1:2, :]
    shift = mod_v[0:1, :]
    base = pl.multiple_of(h * rows, rows)

    def p1_copy(n, c):
        at = pl.ds(pl.multiple_of((1 - n) * 2 * sub + h * sub, sub), sub)
        return pltpu.make_async_remote_copy(
            src_ref=message.at[n, pl.ds(c * sub, sub), :],
            dst_ref=arrived.at[c, at, :],
            send_sem=p1_send.at[n, c],
            recv_sem=p1_recv.at[1 - n, c],
            device_id=nbr_of[n],
            device_id_type=MESH,
        )

    def p1_wait(n, c):
        at = pl.ds(pl.multiple_of(n * 2 * sub + h * sub, sub), sub)
        return pltpu.make_async_remote_copy(
            src_ref=message.at[n, pl.ds(c * sub, sub), :],
            dst_ref=arrived.at[c, at, :],
            send_sem=p1_send.at[n, c],
            recv_sem=p1_recv.at[n, c],
            device_id=nbr_of[n],
            device_id_type=MESH,
        )

    def part_copy(c):
        at = pl.ds(pl.multiple_of(base + c * sub, sub), sub)
        return pltpu.make_async_remote_copy(
            src_ref=normed.at[at, :],
            dst_ref=normed.at[at, :],
            send_sem=part_send.at[c],
            recv_sem=part_recv.at[c],
            device_id=partner,
            device_id_type=MESH,
        )

    def forward_copy(n, c):
        at = pl.ds(pl.multiple_of(n * 2 * sub + h * sub, sub), sub)
        return pltpu.make_async_remote_copy(
            src_ref=arrived.at[c, at, :],
            dst_ref=arrived.at[c, at, :],
            send_sem=f_send.at[n, c],
            recv_sem=f_recv.at[n, c],
            device_id=partner,
            device_id_type=MESH,
        )

    def r_copy(n, c):
        return pltpu.make_async_remote_copy(
            src_ref=r_out.at[n, c],
            dst_ref=r_in.at[1 - n, c],
            send_sem=r_send.at[n, c],
            recv_sem=r_recv.at[1 - n, c],
            device_id=nbr_of[n],
            device_id_type=MESH,
        )

    def t_copy(n, c):
        return pltpu.make_async_remote_copy(
            src_ref=t_out.at[n, c],
            dst_ref=t_in.at[1 - n, c],
            send_sem=t_send.at[n, c],
            recv_sem=t_recv.at[1 - n, c],
            device_id=nbr_of[n],
            device_id_type=MESH,
        )

    for c in range(CHUNKS):
        at = slice(c * sub, (c + 1) * sub)
        hidden = x_v[at, :].astype(F32)
        center = jnp.mean(hidden, axis=-1, keepdims=True)
        shifted = hidden - center
        spread = jnp.mean(shifted * shifted, axis=-1, keepdims=True)
        tokens = (shifted * lax.rsqrt(spread + epsilon) * scale + shift).astype(BF16)
        normed[pl.ds(pl.multiple_of(base + c * sub, sub), sub), :] = tokens
        other = slice(rows + c * sub, rows + (c + 1) * sub)
        packed = jnp.concatenate(
            [stale_v[0, at, half:], stale_v[0, other, half:], stale_v[1, at, half:], stale_v[1, other, half:]], axis=1
        )
        for n in range(2):
            message[n, at, :] = jnp.where(full(gives[n], tokens.shape), tokens, packed)
        if c == 0:
            pl.semaphore_wait(barrier, 3)
        for n in (1, 0):
            p1_copy(n, c).start()
        part_copy(c).start()

    for i in (3, 4, 5):
        loads[i].wait()

    def keep_column(index, part):
        row = keep_v[pl.ds(index * (patch // hd) + part, 1), :]
        return jnp.transpose(jnp.broadcast_to(row.astype(F32), (hd, hd)))

    for part in range(patch // hd):
        column = keep_column(place, part).astype(BF16)
        for group in range(2):
            mbuf[group, part * hd : (part + 1) * hd, :] = column
    live = lax.broadcasted_iota(jnp.int32, (text_rows, hd), 0) < count_s[0]
    text_mask = jnp.where(live, 1.0, 0.0).astype(BF16)
    for group in range(2):
        mbuf[group, patch : patch + text_rows, :] = text_mask
    for n in range(2):
        for part in range(patch // hd):
            column = keep_column((left, right)[n], part)
            seen = (
                jnp.where(full(is_b[n], column.shape), column, 0.0),
                jnp.where(full(is_a[n] + is_b[n], column.shape), column, 0.0),
            )
            for piece in range(hd // sub):
                row = part * hd + piece * sub
                core, c = row // rows, (row % rows) // sub
                to = patch + text_rows + c * keys + n * 2 * sub + core * sub
                for group in range(2):
                    mbuf[group, to : to + sub, :] = seen[group][piece * sub : (piece + 1) * sub].astype(BF16)

    q_gain = gains_v[0:1, :] * (math.log2(math.e) * hd**-0.5)
    k_gain = gains_v[1:2, :]
    t_gain = gains_v[2:3, :]

    for i in range(heads):
        cols = slice(i * hd, (i + 1) * hd)
        kbuf[patch : patch + text_rows, cols] = head_norm(text_v[0, :, cols].astype(F32), t_gain).astype(BF16)
        vbuf[patch : patch + text_rows, cols] = text_v[1, :, cols] * text_mask
    for i in range(half_heads):
        cols = slice(i * hd, (i + 1) * hd)
        kst[:, cols] = head_norm(stale_v[0, :, cols].astype(F32), k_gain).astype(BF16)
        vst[:, cols] = stale_v[1, :, cols] * mbuf[0, :patch, :]

    loads[6].wait()
    wide = 2 * hd

    def project_own(step, carry):
        side = lax.rem(h + step, 2)
        at = pl.ds(pl.multiple_of(side * rows, rows), rows)

        @pl.when(step == 1)
        def _():
            for c in range(CHUNKS):
                spot = pl.ds(pl.multiple_of(side * rows + c * sub, sub), sub)
                pltpu.make_async_remote_copy(
                    src_ref=normed.at[spot, :],
                    dst_ref=normed.at[spot, :],
                    send_sem=part_send.at[c],
                    recv_sem=part_recv.at[c],
                    device_id=partner,
                    device_id_type=MESH,
                ).wait_recv()

        for i in range(local // wide):
            block = slice(i * wide, (i + 1) * wide)
            keys_raw = matmul(normed[at, :], w_v[1, :, block]).astype(BF16)
            fresh_v[0, at, block] = keys_raw
            values_raw = matmul(normed[at, :], w_v[2, :, block]).astype(BF16)
            fresh_v[1, at, block] = values_raw
            queries = matmul(normed[at, :], w_v[0, :, block])
            for j in range(2):
                lanes = slice(j * hd, (j + 1) * hd)
                cols = slice(i * wide + j * hd, i * wide + (j + 1) * hd)
                kbuf[at, cols] = head_norm(keys_raw[:, lanes].astype(F32), k_gain).astype(BF16)
                vbuf[at, cols] = values_raw[:, lanes] * mbuf[0, at, :]
                q_own[at, cols] = head_norm(queries[:, lanes], q_gain).astype(BF16)
        pltpu.make_async_copy(fresh_v.at[:, at, :], fresh_h.at[:, at, :], fresh_sem.at[step]).start()
        return carry

    lax.fori_loop(0, 2, project_own, 0)

    def group_of(i):
        return 0 if i < half_heads else 1

    for i in range(heads):
        cols = slice(i * hd, (i + 1) * hd)
        score = lax.dot_general(q_own[:, cols], kbuf[:patch, cols], NT, preferred_element_type=F32)
        weight = jnp.exp2(score).astype(BF16)
        acc[i] = matmul(weight, jnp.concatenate([vbuf[:patch, cols], mbuf[0, :patch, :]], axis=1))

    def attend(chunk):
        at = pl.ds(pl.multiple_of(chunk * keys, keys), keys)
        for i in range(heads):
            cols = slice(i * hd, (i + 1) * hd)
            score = lax.dot_general(q_own[:, cols], kbuf[at, cols], NT, preferred_element_type=F32)
            weight = jnp.exp2(score).astype(BF16)
            acc[i] += matmul(weight, jnp.concatenate([vbuf[at, cols], mbuf[group_of(i), at, :]], axis=1))

    first = own_chunks + text_rows // keys

    def neighbours(c, carry):
        for n in range(2):
            p1_wait(n, c).wait_recv()
            forward_copy(n, c).start()
        attend(first - 1 + c)
        for n in range(2):
            at = pl.ds(pl.multiple_of(n * 2 * sub + (1 - h) * sub, sub), sub)
            pltpu.make_async_remote_copy(
                src_ref=arrived.at[c, at, :],
                dst_ref=arrived.at[c, at, :],
                send_sem=f_send.at[n, c],
                recv_sem=f_recv.at[n, c],
                device_id=partner,
                device_id_type=MESH,
            ).wait_recv()
        for i in range(half_heads):
            cols = slice(i * hd, (i + 1) * hd)
            nq[:, cols] = head_norm(matmul(arrived[c], w_v[0, :, cols]), q_gain).astype(BF16)
        for i in range(half_heads):
            cols = slice(i * hd, (i + 1) * hd)
            score = lax.dot_general(nq[:, cols], kst[:, cols], NT, preferred_element_type=F32)
            weight = jnp.exp2(score).astype(BF16)
            both = matmul(weight, jnp.concatenate([vst[:, cols], mbuf[0, :patch, :]], axis=1))
            for n in range(2):
                part = slice(n * 2 * sub, (n + 1) * 2 * sub)
                r_out[n, c, :, cols] = both[part, :hd].astype(BF16)
                t_out[n, c, i : i + 1, :] = jnp.transpose(both[part, hd:])[0:1, :]
        for n in range(2):
            r_copy(n, c).start()
            t_copy(n, c).start()
        to = pl.multiple_of((first + c) * keys, keys)
        for i in range(local // wide):
            block = slice(i * wide, (i + 1) * wide)
            keys_raw = matmul(arrived[c], w_v[1, :, block]).astype(BF16)
            values_raw = matmul(arrived[c], w_v[2, :, block]).astype(BF16)
            for j in range(2):
                head = 2 * i + j
                lanes = slice(j * hd, (j + 1) * hd)
                cols = slice(head * hd, (head + 1) * hd)
                for n in range(2):
                    part = slice(n * 2 * sub, (n + 1) * 2 * sub)
                    k_part, v_part = keys_raw[part, lanes], values_raw[part, lanes]
                    if group_of(head) == 1:
                        spot = pl.ds(pl.multiple_of(n * 2 * sub + h * sub, sub), sub)
                        off = (head - half_heads) * hd

                        def sent(index):
                            low = index * half + off
                            return jnp.concatenate(
                                [
                                    arrived[c, spot, low : low + hd],
                                    arrived[c, spot, low + half : low + half + hd],
                                ],
                                axis=0,
                            )

                        pick = full(is_b[n], k_part.shape)
                        k_part = jnp.where(pick, k_part, sent(0))
                        v_part = jnp.where(pick, v_part, sent(2))
                    spot_to = pl.ds(pl.multiple_of(to + n * 2 * sub, 2 * sub), 2 * sub)
                    kbuf[spot_to, cols] = head_norm(k_part.astype(F32), k_gain).astype(BF16)
                    vbuf[spot_to, cols] = v_part * mbuf[group_of(head), spot_to, :]
        return carry

    lax.fori_loop(0, CHUNKS, neighbours, 0)
    attend(first + CHUNKS - 1)

    for i in range(half_heads, heads):
        cols = slice(i * hd, (i + 1) * hd)
        attended[:, cols] = (acc[i, :, :hd] / acc[i, :, hd:]).astype(BF16)

    def combine(c, carry):
        for n in range(2):
            r_copy(1 - n, c).wait_recv()
            t_copy(1 - n, c).wait_recv()
        for i in range(half_heads):
            cols = slice(i * hd, (i + 1) * hd)
            spots = [pl.ds(pl.multiple_of(core * rows + c * sub, sub), sub) for core in range(2)]
            top = jnp.concatenate([acc[i, spot, :hd] for spot in spots], axis=0)
            low = jnp.concatenate([acc[i, spot, hd:] for spot in spots], axis=0)
            for n in range(2):
                pick = full(is_a[n], top.shape)
                total = jnp.transpose(jnp.broadcast_to(t_in[n, c, i : i + 1, :], (hd, 2 * sub)))
                top += jnp.where(pick, r_in[n, c, :, cols].astype(F32), 0.0)
                low += jnp.where(pick, total, 0.0)
            result = (top / low).astype(BF16)
            for core in range(2):
                attended[spots[core], cols] = result[core * sub : (core + 1) * sub]
        return carry

    lax.fori_loop(0, CHUNKS, combine, 0)

    loads[7].wait()
    steps = y_send.shape[0]
    span = width // steps
    other = pl.ds(pl.multiple_of((1 - h) * rows, rows), rows)
    mine = pl.ds(base, rows)

    def y_copy(s):
        cols = pl.ds(pl.multiple_of(s * span, span), span)
        return pltpu.make_async_remote_copy(
            src_ref=y_out.at[:, cols],
            dst_ref=y_in.at[:, cols],
            send_sem=y_send.at[s],
            recv_sem=y_recv.at[s],
            device_id=partner,
            device_id_type=MESH,
        )

    def send_part(s, carry):
        cols = pl.ds(pl.multiple_of(s * span, span), span)
        y_out[:, cols] = matmul(attended[other, :], wo_v[:, cols]).astype(BF16)
        y_copy(s).start()
        return carry

    lax.fori_loop(0, steps, send_part, 0)

    def out_copy(s):
        cols = pl.ds(pl.multiple_of(s * span, span), span)
        return pltpu.make_async_copy(upd_v.at[:, cols], updated_h.at[:, cols], out_sem.at[s])

    def finish(s, carry):
        cols = pl.ds(pl.multiple_of(s * span, span), span)
        mixed = matmul(attended[mine, :], wo_v[:, cols])
        y_copy(s).wait_recv()
        mixed = mixed + y_in[:, cols].astype(F32)
        upd_v[:, cols] = (x_v[:, cols].astype(F32) + mod_v[2:3, cols] * mixed).astype(BF16)
        out_copy(s).start()
        return carry

    lax.fori_loop(0, steps, finish, 0)

    for c in range(CHUNKS):
        for n in range(2):
            p1_copy(n, c).wait_send()
            forward_copy(n, c).wait_send()
            r_copy(n, c).wait_send()
            t_copy(n, c).wait_send()
        part_copy(c).wait_send()
    for s in range(steps):
        y_copy(s).wait_send()
        out_copy(s).wait()
    for step in range(2):
        at = pl.ds(pl.multiple_of(lax.rem(h + step, 2) * rows, rows), rows)
        pltpu.make_async_copy(fresh_v.at[:, at, :], fresh_h.at[:, at, :], fresh_sem.at[step]).wait()


def on_device(
    video_tokens, modulation, project_weight, output_weight, norm_gains,
    text_cache, text_count, video_keep, patch_order, stale_cache,
):
    rows, width = video_tokens.shape
    patch, local = stale_cache.shape[1:]
    hd = norm_gains.shape[1]
    heads = local // hd
    text_rows = text_cache.shape[1]
    half = local // 2
    sub = rows // CHUNKS
    key_rows = 3 * patch + text_rows
    keep = video_keep.reshape(-1, hd)
    y_steps = 3
    anywhere = pl.BlockSpec(memory_space=pl.ANY)
    scalars = pl.BlockSpec(memory_space=pltpu.SMEM)
    dma = pltpu.SemaphoreType.DMA
    vmem = pltpu.VMEM
    return pl.pallas_call(
        kernel,
        out_shape=(
            jax.ShapeDtypeStruct((rows, width), BF16),
            jax.ShapeDtypeStruct((2, patch, local), BF16),
        ),
        in_specs=[scalars, scalars] + [anywhere] * 8,
        out_specs=(anywhere, anywhere),
        scratch_shapes=[
            vmem((rows, width), BF16),
            vmem(modulation.shape, F32),
            vmem(project_weight.shape, BF16),
            vmem(output_weight.shape, BF16),
            vmem(norm_gains.shape, F32),
            vmem(text_cache.shape, BF16),
            vmem(keep.shape, jnp.int32),
            vmem(stale_cache.shape, BF16),
            vmem((patch, width), BF16),
            vmem((2, rows, width), BF16),
            vmem((CHUNKS, 4 * sub, width), BF16),
            vmem((2, patch, local), BF16),
            vmem((patch, local), BF16),
            vmem((key_rows, local), BF16),
            vmem((key_rows, local), BF16),
            vmem((2, key_rows, hd), BF16),
            vmem((patch, half), BF16),
            vmem((patch, half), BF16),
            vmem((4 * sub, half), BF16),
            vmem((heads, patch, 2 * hd), F32),
            vmem((2, CHUNKS, 2 * sub, half), BF16),
            vmem((2, CHUNKS, 2 * sub, half), BF16),
            vmem((2, CHUNKS, 8, 2 * sub), F32),
            vmem((2, CHUNKS, 8, 2 * sub), F32),
            vmem((patch, local), BF16),
            vmem((rows, width), BF16),
            vmem((rows, width), BF16),
            vmem((rows, width), BF16),
            dma((8,)),
            dma((CHUNKS,)),
            dma((CHUNKS,)),
            dma((2, CHUNKS)),
            dma((2, CHUNKS)),
            dma((2, CHUNKS)),
            dma((2, CHUNKS)),
            dma((2, CHUNKS)),
            dma((2, CHUNKS)),
            dma((2, CHUNKS)),
            dma((2, CHUNKS)),
            dma((y_steps,)),
            dma((y_steps,)),
            dma((y_steps,)),
            dma((2,)),
        ],
        compiler_params=pltpu.CompilerParams(
            collective_id=0, has_side_effects=True, vmem_limit_bytes=60 * 1024 * 1024
        ),
        name="patch_attention",
    )(
        patch_order, text_count, video_tokens, modulation, project_weight, output_weight,
        norm_gains, text_cache, keep, stale_cache,
    )


def solution(mesh):
    placed = (
        P(("groups", "section", "head"), None),
        P("groups", None),
        P(None, None, "head"),
        P("head", None),
        P(),
        P(None, "groups", "head"),
        P("groups"),
        P("groups"),
        P("groups"),
        P(None, ("groups", "section"), "head"),
    )
    return jax.shard_map(
        on_device,
        mesh=mesh,
        in_specs=placed,
        out_specs=(P(("groups", "section", "head"), None), P(None, ("groups", "section"), "head")),
        check_vma=False,
    )
```

time: 152 us -> 62.7 us (0.41)
  Pallas kernels: 0 us -> 57.9 us
  local copies, waits for them, and re-layouts: 50.4 us -> 3.33 us
  starting transfers between devices: 31.5 us -> 0 us
  matrix products: 30.9 us -> 0 us
  other arithmetic: 19.3 us -> 0 us
  waiting for transfers between devices: 9.35 us -> 0 us
  blocking collectives: 5.55 us -> 0 us
  between operations: 4.12 us -> 1.3 us
    pallas_call x0 -> x1, Pallas kernels: none -> 57.9 us  [on_device(): pl.pallas_call(kernel, out_shape=(jax.ShapeDtypeStruct((rows, width), BF1...]
    dot_general x4 -> x0, matrix products: 30.9 us -> none  [the longest x1 9.97 us: attend_block(): jnp.einsum('qhd,khd->hqk', queries, key_rows, preferred_element_type=jnp....]
    slice x13 -> x0, local copies, waits for them, and re-layouts: 27.5 us -> none  [the longest x2 5.68 us: on_device(): queries = head_norm(projected[:, :local_width], norm_gains[0])]
    all_to_all x1 -> x0, starting transfers between devices: 25 us -> none  [copy_for_each(): return lax.all_to_all(copies, axis, split_axis=0, concat_axis=0, tiled=True)]
    unnamed x32 -> x4, local copies, waits for them, and re-layouts: 13.1 us -> 3.33 us
    ppermute x2 -> x0, waiting for transfers between devices: 9.35 us -> none  [from_behind(): return lax.ppermute(array, axis, pairs)]
    reduce_sum x7 -> x0, other arithmetic: 8.44 us -> none  [the longest x3 4.52 us: head_norm(): jnp.mean(per_head * per_head, axis=-1, keepdims=True) + epsilon]
    ppermute x2 -> x0, starting transfers between devices: 6.48 us -> none  [from_behind(): return lax.ppermute(array, axis, pairs)]
  transfers between devices with their start and end apart: 3 -> 0, of which waited for: 1 -> 0; matrix products, arithmetic and copies ran while one was open for 28% -> 0% of each run, Pallas kernels for 0% -> 0%
where the time goes in v1:
time: 62.7 us; the launch traced here: 62.5 us
  Pallas kernels  57.9 us (92%)
  local copies, waits for them, and re-layouts  3.33 us (5%)
  between operations  1.3 us (2%)
    pallas_call x1, Pallas kernels, on_device(): pl.pallas_call(kernel, out_shape=(jax.ShapeDtypeStruct((rows, width), BF1...  57.9 us
    unnamed x4, local copies, waits for them, and re-layouts  3.33 us

profile of v1, /device:TPU:513, one launch (start us, length us, event | category | flops | bytes accessed | tf_op | source)
XLA Modules:
  0.0 62.5 jit_solution(15344176256003287517)
XLA Ops:
  1.3 57.9 %patch_attention.1 = (bf16[256,1536]{1,0:T(8,128)(2,1)}, bf16[2,512,768]{2,1,0:T(8,128)(2,1)}) custom-call(s32[64]{0:T(128)} %order_s.1, s32[1]{0:T(128)S(6)} %copy.14.count_s, bf16[256,1536]{1,0:T(8,128)(2,1)} %x_h.1, f32[3,1536]{1,0:T(4,128)} %mod_h.1, bf16[3,1536,768]{2,1,0:T(8,128)(2,1)} %w_h.1, bf16[768,1536]{1,0:T(8,128)(2,1)} %wo_h.1, ...), custom_call_target="tpu_custom_call" | custom-call | tf_op jit(solution)/shard_map/patch_attention/pallas_call | solution.py:437
  59.2 0.0 copy-start
  59.2 2.2 %copy.15 = bf16[256,1536]{1,0:T(8,128)(2,1)} copy(bf16[256,1536]{1,0:T(8,128)(2,1)} %get-tuple-element.4) | data formatting | bytes 1572864
  61.4 0.0 copy-done
  61.4 1.1 %copy.16 = bf16[2,512,768]{2,1,0:T(8,128)(2,1)} copy(bf16[2,512,768]{2,1,0:T(8,128)(2,1)S(1)} %copy-done) | data formatting | bytes 3145728
Async XLA Ops:
  59.2 2.2 %copy-start = (bf16[2,512,768]{2,1,0:T(8,128)(2,1)S(1)}, bf16[2,512,768]{2,1,0:T(8,128)(2,1)}, u32[]{:S(2)}) copy-start(bf16[2,512,768]{2,1,0:T(8,128)(2,1)} %get-tuple-element.5) | copy-start | bytes 4718596

commit v2 on v0

v2 whole, which is shorter than its diff:
```python
import functools
import math

import jax
import jax.numpy as jnp
from jax import lax
from jax.experimental import pallas as pl
from jax.experimental.pallas import tpu as pltpu
from jax.sharding import PartitionSpec as P

epsilon = 1e-06
CHUNKS = 2
F32 = jnp.float32
BF16 = jnp.bfloat16
MESH = pl.DeviceIdType.MESH
NT = (((1,), (1,)), ((), ()))


def matmul(a, b):
    return jnp.dot(a, b, preferred_element_type=F32)


def head_norm(values, gain):
    square = jnp.mean(values * values, axis=-1, keepdims=True)
    return values * lax.rsqrt(square + epsilon) * gain


def kernel(
    order_s, count_s, x_h, mod_h, w_h, wo_h, gains_h, text_h, keep_h, stale_h,
    updated_h, fresh_h,
    x_v, mod_v, w_v, wo_v, gains_v, text_v, keep_v, stale_v,
    normed, message, arrived, extra, raw, q_own, kbuf, vbuf, mbuf, acc, attended, y_sum, y_out, y_in, fresh_v, updated_v,
    load_sem, part_send, part_recv, p1_send, p1_recv, f_send, f_recv, e_send, e_recv, y_send, y_recv, out_sem,
    left_ready, partner_ready,
):
    rows, width = x_v.shape
    patch, local = stale_v.shape[1], stale_v.shape[2]
    text_rows = text_v.shape[1]
    hd = gains_v.shape[1]
    heads = local // hd
    half_heads = heads // 2
    half = half_heads * hd
    sub = rows // CHUNKS
    wide = 2 * hd
    sections = lax.axis_size("section")
    place = lax.axis_index("section")
    h = lax.axis_index("head")
    nbr_place = (jnp.maximum(place - 1, 0), jnp.minimum(place + 1, sections - 1))
    nbr_of = ({"section": nbr_place[0]}, {"section": nbr_place[1]})
    partner = {"head": 1 - h}
    exists = (place > 0, place < sections - 1)
    inner = (place > 0) & (place < sections - 1)

    def for_neighbour(n, work):
        pl.when(exists[n])(work)

    barrier = pltpu.get_barrier_semaphore()
    for_neighbour(0, lambda: pl.semaphore_signal(barrier, inc=1, device_id=nbr_of[0], device_id_type=MESH))

    @pl.when(h == 1)
    def _():
        pl.semaphore_signal(barrier, inc=1, device_id=partner, device_id_type=MESH)

    sources = [
        (x_h, x_v), (mod_h, mod_v), (stale_h, stale_v), (gains_h, gains_v), (keep_h, keep_v),
        (w_h.at[1], w_v.at[1]), (w_h.at[2], w_v.at[2]), (w_h.at[0], w_v.at[0]), (text_h, text_v), (wo_h, wo_v),
    ]
    loads = [pltpu.make_async_copy(src, dst, load_sem.at[i]) for i, (src, dst) in enumerate(sources)]
    for load in loads:
        load.start()

    own_slot = order_s[place]
    slot = (order_s[nbr_place[0]], order_s[nbr_place[1]])
    one = jnp.int32(1)
    zero = jnp.int32(0)
    is_b = [jnp.where(slot[n] < own_slot, one, zero) for n in range(2)]
    is_a = [jnp.where(own_slot < slot[n], one, zero) for n in range(2)]

    def full(flag, shape):
        return jnp.full(shape, flag, jnp.int32) > 0

    base = pl.multiple_of(h * rows, rows)

    def area(n, core):
        return pl.ds(pl.multiple_of((2 * n + core) * sub, sub), sub)

    def p1_copy(n, c, side):
        at = pl.ds(pl.multiple_of(c * sub, sub), sub)
        return pltpu.make_async_remote_copy(
            src_ref=message.at[n, at, :],
            dst_ref=arrived.at[c, area(side, h), :],
            send_sem=p1_send.at[n, c],
            recv_sem=p1_recv.at[side, c],
            device_id=nbr_of[n],
            device_id_type=MESH,
        )

    def extra_copy(n, kind, i, side):
        cols = slice(i * hd, (i + 1) * hd)
        return pltpu.make_async_remote_copy(
            src_ref=stale_v.at[kind, :, cols],
            dst_ref=extra.at[side, kind, :, cols],
            send_sem=e_send.at[n, kind, i],
            recv_sem=e_recv.at[side, kind, i],
            device_id=nbr_of[n],
            device_id_type=MESH,
        )

    def part_copy(c, core):
        at = pl.ds(pl.multiple_of(core * rows + c * sub, sub), sub)
        return pltpu.make_async_remote_copy(
            src_ref=normed.at[at, :],
            dst_ref=normed.at[at, :],
            send_sem=part_send.at[c],
            recv_sem=part_recv.at[c],
            device_id=partner,
            device_id_type=MESH,
        )

    def forward_copy(n, c, core):
        return pltpu.make_async_remote_copy(
            src_ref=arrived.at[c, area(n, core), :],
            dst_ref=arrived.at[c, area(n, core), :],
            send_sem=f_send.at[n, c],
            recv_sem=f_recv.at[n, c],
            device_id=partner,
            device_id_type=MESH,
        )

    extras = [(kind, i) for i in range(half_heads) for kind in range(2)]

    def send_extras(n):
        for kind, i in extras:
            extra_copy(n, kind, i, 1 - n).start()

    def meet_left():
        pl.semaphore_wait(left_ready, 1)
        for c in range(CHUNKS):
            p1_copy(0, c, 1).start()

    def swap_parts():
        for c in range(CHUNKS):
            part_copy(c, h).start()

    def meet_right():
        needed = jnp.where(place < sections - 1, one, zero) + jnp.where(h == 0, one, zero)
        pl.when(needed > 0)(lambda: pl.semaphore_wait(barrier, needed))
        for_neighbour(1, lambda: pl.semaphore_signal(left_ready, inc=1, device_id=nbr_of[1], device_id_type=MESH))

        @pl.when(h == 0)
        def _():
            pl.semaphore_signal(partner_ready, inc=1, device_id=partner, device_id_type=MESH)

    def meet_partner():
        pl.semaphore_wait(partner_ready, 1)
        swap_parts()

    loads[0].wait()
    loads[1].wait()
    scale = 1.0 + mod_v[1:2, :]
    shift = mod_v[0:1, :]
    piece = sub // 2
    for c in range(CHUNKS):
        for p in range(2):
            at = slice(c * sub + p * piece, c * sub + (p + 1) * piece)
            hidden = x_v[at, :].astype(F32)
            center = jnp.mean(hidden, axis=-1, keepdims=True)
            shifted = hidden - center
            spread = jnp.mean(shifted * shifted, axis=-1, keepdims=True)
            tokens = (shifted * lax.rsqrt(spread + epsilon) * scale + shift).astype(BF16)
            normed[pl.ds(pl.multiple_of(base + c * sub + p * piece, piece), piece), :] = tokens
            if c == 0 and p == 0:
                meet_right()
                loads[2].wait()
            other = slice(rows + c * sub + p * piece, rows + c * sub + (p + 1) * piece)
            packed = jnp.concatenate(
                [stale_v[0, at, half:], stale_v[0, other, half:], stale_v[1, at, half:], stale_v[1, other, half:]],
                axis=1,
            )
            for n in range(2):
                message[n, at, :] = jnp.where(full(is_a[n], tokens.shape), tokens, packed)
        for_neighbour(1, lambda c=c: p1_copy(1, c, 0).start())

    waits = (place == 1) & (h == 0)
    pl.when((place > 0) & jnp.logical_not(waits))(meet_left)
    pl.when(h == 0)(swap_parts)
    pl.when((h == 1) & (place > 0))(meet_partner)

    for i in (3, 4):
        loads[i].wait()
    near = patch + text_rows

    def keep_column(index, part):
        row = keep_v[pl.ds(index * (patch // hd) + part, 1), :]
        return jnp.transpose(jnp.broadcast_to(row.astype(F32), (hd, hd))).astype(BF16)

    for part in range(patch // hd):
        low = part * hd
        mbuf[low : low + hd, :] = keep_column(place, part)
        for n in range(2):
            mbuf[near + n * patch + low : near + n * patch + low + hd, :] = keep_column(nbr_place[n], part)
    live = lax.broadcasted_iota(jnp.int32, (text_rows, hd), 0) < count_s[0]
    mbuf[patch:near, :] = jnp.where(live, 1.0, 0.0).astype(BF16)

    q_gain = gains_v[0:1, :] * (math.log2(math.e) * hd**-0.5)
    k_gain = gains_v[1:2, :]
    t_gain = gains_v[2:3, :]

    def own(at, index, beside):
        for i in range(local // wide):
            block = slice(i * wide, (i + 1) * wide)
            result = matmul(normed[at, :], w_v[index, :, block])
            if index > 0:
                result = result.astype(BF16)
                fresh_v[index - 1, at, block] = result
            for j in range(2):
                lanes = slice(j * hd, (j + 1) * hd)
                cols = slice(i * wide + j * hd, i * wide + (j + 1) * hd)
                if index == 0:
                    q_own[at, cols] = head_norm(result[:, lanes], q_gain).astype(BF16)
                if index == 1:
                    kbuf[at, cols] = head_norm(result[:, lanes].astype(F32), k_gain).astype(BF16)
                if index == 2:
                    vbuf[at, cols] = result[:, lanes] * mbuf[at, :]
                if beside:
                    kbuf[patch:near, cols] = head_norm(text_v[0, :, cols].astype(F32), t_gain).astype(BF16)
                    vbuf[patch:near, cols] = text_v[1, :, cols] * mbuf[patch:near, :]

    for step in range(2):
        side = h if step == 0 else 1 - h
        at = pl.ds(pl.multiple_of(side * rows, rows), rows)
        if step == 1:
            for_neighbour(1, lambda: send_extras(1))
            pl.when((h == 1) & (place == 0))(meet_partner)
            pl.when((place > 0) & jnp.logical_not(waits))(lambda: send_extras(0))
            for c in range(CHUNKS):
                part_copy(c, 1 - h).wait_recv()
        for index in (1, 2, 0):
            if step == 0:
                loads[{1: 5, 2: 6, 0: 7}[index]].wait()
            if step == 1 and index == 1:
                loads[8].wait()
            own(at, index, step == 1 and index == 1)
        pltpu.make_async_copy(fresh_v.at[:, at, :], fresh_h.at[:, at, :], out_sem.at[step]).start()

    def take(n, c):
        p1_copy(n, c, n).wait_recv()
        forward_copy(n, c, h).start()

    def scores(query, key):
        return lax.dot_general(query, key, NT, preferred_element_type=F32)

    def attend(at, i):
        cols = slice(i * hd, (i + 1) * hd)
        weight = jnp.exp2(scores(q_own[:, cols], kbuf[at, cols])).astype(BF16)
        return matmul(weight, jnp.concatenate([vbuf[at, cols], mbuf[at, :]], axis=1))

    for i in range(heads):
        acc[i] = attend(slice(0, near), i)

    def job(n, c):
        forward_copy(n, c, 1 - h).wait_recv()
        tokens = arrived.at[c, pl.ds(2 * n * sub, 2 * sub), :]
        pick = full(is_b[n], (sub, hd))
        for i in reversed(range(local // wide)):
            block = slice(i * wide, (i + 1) * wide)
            for kind in range(2):
                result = matmul(tokens[...], w_v[1 + kind, :, block]).astype(BF16)
                for j in range(2):
                    head = 2 * i + j
                    cols = slice(head * hd, (head + 1) * hd)
                    for core in range(2):
                        part = result[core * sub : (core + 1) * sub, j * hd : (j + 1) * hd]
                        row = pl.multiple_of(core * rows + c * sub, sub)
                        if head < half_heads:
                            raw[n, kind, pl.ds(row, sub), cols] = part
                            continue
                        low = (2 * kind + core) * half + (head - half_heads) * hd
                        part = jnp.where(pick, part, arrived[c, area(n, h), low : low + hd])
                        to = pl.ds(pl.multiple_of(near + n * patch + row, sub), sub)
                        if kind == 0:
                            kbuf[to, cols] = head_norm(part.astype(F32), k_gain).astype(BF16)
                        else:
                            vbuf[to, cols] = part * mbuf[to, :]

    def take_left(chunks):
        for c in chunks:
            take(0, c)

    ready = (place > 0) & jnp.logical_not(waits)
    for c in range(CHUNKS):
        for_neighbour(1, lambda: take(1, c))
        pl.when(ready)(lambda: take(0, c))
        for_neighbour(1, lambda: job(1, c))
        if c == 0:

            @pl.when(waits)
            def _():
                meet_left()
                send_extras(0)

    pl.when(waits)(lambda: take_left(range(CHUNKS)))

    @pl.when(exists[0])
    def _():
        for c in range(CHUNKS):
            job(0, c)

    def finish_head(at, i):
        cols = slice(i * hd, (i + 1) * hd)
        both = acc[i] + attend(at, i)
        attended[:, cols] = (both[:, :hd] / both[:, hd:]).astype(BF16)

    def finish_heads(which):
        @pl.when(inner)
        def _():
            for i in which:
                finish_head(slice(near, near + 2 * patch), i)

        @pl.when(jnp.logical_not(inner))
        def _():
            at = pl.ds(pl.multiple_of(near + jnp.where(place > 0, 0, patch), 2 * sub), patch)
            for i in which:
                finish_head(at, i)

    def take_extra(n, i):
        for kind in range(2):
            extra_copy(n, kind, i, n).wait_recv()
        cols = slice(i * hd, (i + 1) * hd)
        pick = full(is_b[n], (patch, hd))
        to = slice(near + n * patch, near + (n + 1) * patch)
        k_part = jnp.where(pick, raw[n, 0, :, cols], extra[n, 0, :, cols])
        v_part = jnp.where(pick, raw[n, 1, :, cols], extra[n, 1, :, cols])
        kbuf[to, cols] = head_norm(k_part.astype(F32), k_gain).astype(BF16)
        vbuf[to, cols] = v_part * mbuf[to, :]

    def extra_head(i):
        for n in (1, 0):
            for_neighbour(n, lambda n=n: take_extra(n, i))
        finish_heads([i])

    steps = y_send.shape[0]
    span = width // steps

    def partial_sum(pair, first):
        lanes = slice(pair * wide, (pair + 1) * wide)
        for s in range(steps):
            cols = slice(s * span, (s + 1) * span)
            part = matmul(attended[:, lanes], wo_v[lanes, cols])
            y_sum[:, cols] = part if first else y_sum[:, cols] + part

    finish_heads(range(half_heads, heads))
    loads[9].wait()
    last = (half_heads - 1) // 2
    late_pairs = [pair for pair in range(heads // 2) if 2 * pair + 1 < half_heads]
    early_pairs = [pair for pair in range(heads // 2) if 2 * pair >= half_heads]
    for k, pair in enumerate(early_pairs):
        partial_sum(pair, k == 0)
    for i in range(half_heads - 1):
        extra_head(i)
    for pair in late_pairs:
        partial_sum(pair, False)
    extra_head(half_heads - 1)

    lanes = slice(last * wide, (last + 1) * wide)
    other = pl.ds(pl.multiple_of((1 - h) * rows, rows), rows)
    mine = pl.ds(base, rows)

    def y_copy(s):
        cols = slice(s * span, (s + 1) * span)
        return pltpu.make_async_remote_copy(
            src_ref=y_out.at[:, cols],
            dst_ref=y_in.at[:, cols],
            send_sem=y_send.at[s],
            recv_sem=y_recv.at[s],
            device_id=partner,
            device_id_type=MESH,
        )

    for s in range(steps):
        cols = slice(s * span, (s + 1) * span)
        y_out[:, cols] = (y_sum[other, cols] + matmul(attended[other, lanes], wo_v[lanes, cols])).astype(BF16)
        y_copy(s).start()
    for s in range(steps):
        cols = slice(s * span, (s + 1) * span)
        y_sum[mine, cols] += matmul(attended[mine, lanes], wo_v[lanes, cols])
    for s in range(steps):
        cols = slice(s * span, (s + 1) * span)
        y_copy(s).wait_recv()
        mixed = y_sum[mine, cols] + y_in[:, cols].astype(F32)
        updated_v[:, cols] = (x_v[:, cols].astype(F32) + mod_v[2:3, cols] * mixed).astype(BF16)
        pltpu.make_async_copy(updated_v.at[:, cols], updated_h.at[:, cols], out_sem.at[2 + s]).start()

    def sent_to(n):
        for c in range(CHUNKS):
            p1_copy(n, c, 1 - n).wait_send()
            forward_copy(n, c, h).wait_send()
        for kind, i in extras:
            extra_copy(n, kind, i, 1 - n).wait_send()

    for n in range(2):
        for_neighbour(n, lambda n=n: sent_to(n))
    for c in range(CHUNKS):
        part_copy(c, h).wait_send()
    for s in range(steps):
        y_copy(s).wait_send()
        cols = slice(s * span, (s + 1) * span)
        pltpu.make_async_copy(updated_v.at[:, cols], updated_h.at[:, cols], out_sem.at[2 + s]).wait()
    for step in range(2):
        at = pl.ds(pl.multiple_of(jnp.where(step == 0, h, 1 - h) * rows, rows), rows)
        pltpu.make_async_copy(fresh_v.at[:, at, :], fresh_h.at[:, at, :], out_sem.at[step]).wait()


def on_device(
    video_tokens, modulation, project_weight, output_weight, norm_gains,
    text_cache, text_count, video_keep, patch_order, stale_cache,
):
    rows, width = video_tokens.shape
    patch, local = stale_cache.shape[1:]
    hd = norm_gains.shape[1]
    heads = local // hd
    text_rows = text_cache.shape[1]
    half = local // 2
    sub = rows // CHUNKS
    key_rows = 3 * patch + text_rows
    keep = video_keep.reshape(-1, hd)
    y_steps = 3
    anywhere = pl.BlockSpec(memory_space=pl.ANY)
    scalars = pl.BlockSpec(memory_space=pltpu.SMEM)
    dma = pltpu.SemaphoreType.DMA
    vmem = pltpu.VMEM
    return pl.pallas_call(
        kernel,
        out_shape=(
            jax.ShapeDtypeStruct((rows, width), BF16),
            jax.ShapeDtypeStruct((2, patch, local), BF16),
        ),
        in_specs=[scalars, scalars] + [anywhere] * 8,
        out_specs=(anywhere, anywhere),
        scratch_shapes=[
            vmem((rows, width), BF16),
            vmem(modulation.shape, F32),
            vmem(project_weight.shape, BF16),
            vmem(output_weight.shape, BF16),
            vmem(norm_gains.shape, F32),
            vmem(text_cache.shape, BF16),
            vmem(keep.shape, jnp.int32),
            vmem(stale_cache.shape, BF16),
            vmem((patch, width), BF16),
            vmem((2, rows, width), BF16),
            vmem((CHUNKS, 4 * sub, width), BF16),
            vmem((2, 2, patch, half), BF16),
            vmem((2, 2, patch, half), BF16),
            vmem((patch, local), BF16),
            vmem((key_rows, local), BF16),
            vmem((key_rows, local), BF16),
            vmem((key_rows, hd), BF16),
            vmem((heads, patch, 2 * hd), F32),
            vmem((patch, local), BF16),
            vmem((patch, width), F32),
            vmem((rows, width), BF16),
            vmem((rows, width), BF16),
            vmem((2, patch, local), BF16),
            vmem((rows, width), BF16),
            dma((10,)),
            dma((CHUNKS,)),
            dma((CHUNKS,)),
            dma((2, CHUNKS)),
            dma((2, CHUNKS)),
            dma((2, CHUNKS)),
            dma((2, CHUNKS)),
            dma((2, 2, heads // 2)),
            dma((2, 2, heads // 2)),
            dma((y_steps,)),
            dma((y_steps,)),
            dma((2 + y_steps,)),
            pltpu.SemaphoreType.REGULAR,
            pltpu.SemaphoreType.REGULAR,
        ],
        compiler_params=pltpu.CompilerParams(
            collective_id=0, has_side_effects=True, vmem_limit_bytes=60 * 1024 * 1024
        ),
        name="patch_attention",
    )(
        patch_order, text_count, video_tokens, modulation, project_weight, output_weight,
        norm_gains, text_cache, keep, stale_cache,
    )


def solution(mesh):
    placed = (
        P(("groups", "section", "head"), None),
        P("groups", None),
        P(None, None, "head"),
        P("head", None),
        P(),
        P(None, "groups", "head"),
        P("groups"),
        P("groups"),
        P("groups"),
        P(None, ("groups", "section"), "head"),
    )
    return jax.shard_map(
        on_device,
        mesh=mesh,
        in_specs=placed,
        out_specs=(P(("groups", "section", "head"), None), P(None, ("groups", "section"), "head")),
        check_vma=False,
    )
```

time: 152 us -> 52.9 us (0.35)
  the two profiles are of different devices: /device:TPU:513 before, /device:TPU:575 now
where the time goes in v2:
time: 52.9 us; the launch traced here: 52.7 us
  Pallas kernels  48.1 us (91%)
  local copies, waits for them, and re-layouts  3.33 us (6%)
  between operations  1.3 us (2%)
    pallas_call x1, Pallas kernels, on_device(): pl.pallas_call(kernel, out_shape=(jax.ShapeDtypeStruct((rows, width), BF1...  48.1 us
    unnamed x4, local copies, waits for them, and re-layouts  3.33 us

profile of v2, /device:TPU:575, one launch (start us, length us, event | category | flops | bytes accessed | tf_op | source)
XLA Modules:
  0.0 52.7 jit_solution(747621616756781184)
XLA Ops:
  1.3 48.1 %patch_attention.1 = (bf16[256,1536]{1,0:T(8,128)(2,1)}, bf16[2,512,768]{2,1,0:T(8,128)(2,1)}) custom-call(s32[64]{0:T(128)} %order_s.1, s32[1]{0:T(128)S(6)} %copy.14.count_s, bf16[256,1536]{1,0:T(8,128)(2,1)} %x_h.1, f32[3,1536]{1,0:T(4,128)} %mod_h.1, bf16[3,1536,768]{2,1,0:T(8,128)(2,1)} %w_h.1, bf16[768,1536]{1,0:T(8,128)(2,1)} %wo_h.1, ...), custom_call_target="tpu_custom_call" | custom-call | tf_op jit(solution)/shard_map/patch_attention/pallas_call | solution.py:432
  49.4 0.0 copy-start
  49.4 2.2 %copy.15 = bf16[256,1536]{1,0:T(8,128)(2,1)} copy(bf16[256,1536]{1,0:T(8,128)(2,1)} %get-tuple-element.4) | data formatting | bytes 1572864
  51.6 0.0 copy-done
  51.6 1.1 %copy.16 = bf16[2,512,768]{2,1,0:T(8,128)(2,1)} copy(bf16[2,512,768]{2,1,0:T(8,128)(2,1)S(1)} %copy-done) | data formatting | bytes 3145728
Async XLA Ops:
  49.4 2.2 %copy-start = (bf16[2,512,768]{2,1,0:T(8,128)(2,1)S(1)}, bf16[2,512,768]{2,1,0:T(8,128)(2,1)}, u32[]{:S(2)}) copy-start(bf16[2,512,768]{2,1,0:T(8,128)(2,1)} %get-tuple-element.5) | copy-start | bytes 4718596

commit v3 on v2

--- a/solution.py
+++ b/solution.py
@@ -26,10 +26,10 @@
 
 
 def kernel(
-    order_s, count_s, x_h, mod_h, w_h, wo_h, gains_h, text_h, keep_h, stale_h,
+    order_h, count_h, x_h, mod_h, w_h, wo_h, gains_h, text_h, keep_h, stale_h,
     updated_h, fresh_h,
     x_v, mod_v, w_v, wo_v, gains_v, text_v, keep_v, stale_v,
-    normed, message, arrived, extra, raw, q_own, kbuf, vbuf, mbuf, acc, attended, y_sum, y_out, y_in, fresh_v, updated_v,
+    normed, message, arrived, extra, raw, q_own, kbuf, vbuf, mbuf, acc, attended, y_sum, y_out, y_in, fresh_v, updated_v, order_s, count_s,
     load_sem, part_send, part_recv, p1_send, p1_recv, f_send, f_recv, e_send, e_recv, y_send, y_recv, out_sem,
     left_ready, partner_ready,
 ):
@@ -62,19 +62,18 @@
         pl.semaphore_signal(barrier, inc=1, device_id=partner, device_id_type=MESH)
 
     sources = [
-        (x_h, x_v), (mod_h, mod_v), (stale_h, stale_v), (gains_h, gains_v), (keep_h, keep_v),
-        (w_h.at[1], w_v.at[1]), (w_h.at[2], w_v.at[2]), (w_h.at[0], w_v.at[0]), (text_h, text_v), (wo_h, wo_v),
+        (order_h, order_s), (mod_h, mod_v), (stale_h, stale_v), (gains_h, gains_v), (keep_h, keep_v),
+        (w_h.at[1], w_v.at[1]), (w_h.at[2], w_v.at[2]), (w_h.at[0], w_v.at[0]), (text_h, text_v), (wo_h, wo_v), (count_h, count_s),
     ]
+    piece = sub // 2
+    sources += [(x_h.at[pl.ds(i * piece, piece), :], x_v.at[pl.ds(i * piece, piece), :]) for i in range(2 * CHUNKS)]
+    first_piece = len(sources) - 2 * CHUNKS
     loads = [pltpu.make_async_copy(src, dst, load_sem.at[i]) for i, (src, dst) in enumerate(sources)]
-    for load in loads:
-        load.start()
-
-    own_slot = order_s[place]
-    slot = (order_s[nbr_place[0]], order_s[nbr_place[1]])
+    for i in (*range(first_piece, len(loads)), *range(first_piece)):
+        loads[i].start()
+
     one = jnp.int32(1)
     zero = jnp.int32(0)
-    is_b = [jnp.where(slot[n] < own_slot, one, zero) for n in range(2)]
-    is_a = [jnp.where(own_slot < slot[n], one, zero) for n in range(2)]
 
     def full(flag, shape):
         return jnp.full(shape, flag, jnp.int32) > 0
@@ -155,14 +154,18 @@
         pl.semaphore_wait(partner_ready, 1)
         swap_parts()
 
+    loads[1].wait()
     loads[0].wait()
-    loads[1].wait()
+    own_slot = order_s[place]
+    slot = (order_s[nbr_place[0]], order_s[nbr_place[1]])
+    is_b = [jnp.where(slot[n] < own_slot, one, zero) for n in range(2)]
+    is_a = [jnp.where(own_slot < slot[n], one, zero) for n in range(2)]
     scale = 1.0 + mod_v[1:2, :]
     shift = mod_v[0:1, :]
-    piece = sub // 2
     for c in range(CHUNKS):
         for p in range(2):
             at = slice(c * sub + p * piece, c * sub + (p + 1) * piece)
+            loads[first_piece + 2 * c + p].wait()
             hidden = x_v[at, :].astype(F32)
             center = jnp.mean(hidden, axis=-1, keepdims=True)
             shifted = hidden - center
@@ -186,7 +189,7 @@
     pl.when(h == 0)(swap_parts)
     pl.when((h == 1) & (place > 0))(meet_partner)
 
-    for i in (3, 4):
+    for i in (3, 4, 10):
         loads[i].wait()
     near = patch + text_rows
 
@@ -255,6 +258,7 @@
         weight = jnp.exp2(scores(q_own[:, cols], kbuf[at, cols])).astype(BF16)
         return matmul(weight, jnp.concatenate([vbuf[at, cols], mbuf[at, :]], axis=1))
 
+    pl.when(place == 0)(lambda: take(1, 0))
     for i in range(heads):
         acc[i] = attend(slice(0, near), i)
 
@@ -283,28 +287,29 @@
                         else:
                             vbuf[to, cols] = part * mbuf[to, :]
 
-    def take_left(chunks):
-        for c in chunks:
-            take(0, c)
-
-    ready = (place > 0) & jnp.logical_not(waits)
-    for c in range(CHUNKS):
-        for_neighbour(1, lambda: take(1, c))
-        pl.when(ready)(lambda: take(0, c))
-        for_neighbour(1, lambda: job(1, c))
-        if c == 0:
-
-            @pl.when(waits)
-            def _():
-                meet_left()
-                send_extras(0)
-
-    pl.when(waits)(lambda: take_left(range(CHUNKS)))
-
-    @pl.when(exists[0])
-    def _():
-        for c in range(CHUNKS):
-            job(0, c)
+    def jobs(t, carry):
+        delay = jnp.where(place == 1, CHUNKS, 0)
+        has_right = exists[1] & (t < CHUNKS)
+        has_left = exists[0] & (t >= delay) & (t < delay + CHUNKS)
+
+        @pl.when(waits & (t == 1))
+        def _():
+            meet_left()
+            send_extras(0)
+
+        pl.when(has_right & (place > 0))(lambda: take(1, t))
+        pl.when(has_left)(lambda: take(0, t - delay))
+
+        @pl.when((place == 0) & (t == 0))
+        def _():
+            for c in range(1, CHUNKS):
+                take(1, c)
+
+        pl.when(has_right)(lambda: job(1, t))
+        pl.when(has_left)(lambda: job(0, t - delay))
+        return carry
+
+    lax.fori_loop(0, 2 * CHUNKS, jobs, 0)
 
     def finish_head(at, i):
         cols = slice(i * hd, (i + 1) * hd)
@@ -426,7 +431,6 @@
     keep = video_keep.reshape(-1, hd)
     y_steps = 3
     anywhere = pl.BlockSpec(memory_space=pl.ANY)
-    scalars = pl.BlockSpec(memory_space=pltpu.SMEM)
     dma = pltpu.SemaphoreType.DMA
     vmem = pltpu.VMEM
     return pl.pallas_call(
@@ -435,7 +439,7 @@
             jax.ShapeDtypeStruct((rows, width), BF16),
             jax.ShapeDtypeStruct((2, patch, local), BF16),
         ),
-        in_specs=[scalars, scalars] + [anywhere] * 8,
+        in_specs=[anywhere] * 10,
         out_specs=(anywhere, anywhere),
         scratch_shapes=[
             vmem((rows, width), BF16),
@@ -462,7 +466,9 @@
             vmem((rows, width), BF16),
             vmem((2, patch, local), BF16),
             vmem((rows, width), BF16),
-            dma((10,)),
+            pltpu.SMEM(patch_order.shape, jnp.int32),
+            pltpu.SMEM(text_count.shape, jnp.int32),
+            dma((11 + 2 * CHUNKS,)),
             dma((CHUNKS,)),
             dma((CHUNKS,)),
             dma((2, CHUNKS)),

time: 52.9 us -> 52.2 us (0.987)
  the two profiles are of different devices: /device:TPU:575 before, /device:TPU:703 now
where the time goes in v3:
time: 52.2 us; the launch traced here: 52.1 us
  Pallas kernels  47.5 us (91%)
  local copies, waits for them, and re-layouts  3.33 us (6%)
  between operations  1.3 us (2%)
    pallas_call x1, Pallas kernels, on_device(): pl.pallas_call(kernel, out_shape=(jax.ShapeDtypeStruct((rows, width), BF1...  47.5 us
    unnamed x4, local copies, waits for them, and re-layouts  3.33 us

profile of v3, /device:TPU:703, one launch (start us, length us, event | category | flops | bytes accessed | tf_op | source)
XLA Modules:
  0.0 52.1 jit_solution(17241016570703679652)
XLA Ops:
  1.3 47.5 %patch_attention.1 = (bf16[256,1536]{1,0:T(8,128)(2,1)}, bf16[2,512,768]{2,1,0:T(8,128)(2,1)}) custom-call(s32[64]{0:T(128)} %order_h.1, s32[1]{0:T(128)S(6)} %copy.14.count_h, bf16[256,1536]{1,0:T(8,128)(2,1)} %x_h.1, f32[3,1536]{1,0:T(4,128)} %mod_h.1, bf16[3,1536,768]{2,1,0:T(8,128)(2,1)} %w_h.1, bf16[768,1536]{1,0:T(8,128)(2,1)} %wo_h.1, ...), custom_call_target="tpu_custom_call" | custom-call | tf_op jit(solution)/shard_map/patch_attention/pallas_call | solution.py:436
  48.8 0.0 copy-start
  48.8 2.2 %copy.15 = bf16[256,1536]{1,0:T(8,128)(2,1)} copy(bf16[256,1536]{1,0:T(8,128)(2,1)} %get-tuple-element.4) | data formatting | bytes 1572864
  51.0 0.0 copy-done
  51.0 1.1 %copy.16 = bf16[2,512,768]{2,1,0:T(8,128)(2,1)} copy(bf16[2,512,768]{2,1,0:T(8,128)(2,1)S(1)} %copy-done) | data formatting | bytes 3145728
Async XLA Ops:
  48.8 2.2 %copy-start = (bf16[2,512,768]{2,1,0:T(8,128)(2,1)S(1)}, bf16[2,512,768]{2,1,0:T(8,128)(2,1)}, u32[]{:S(2)}) copy-start(bf16[2,512,768]{2,1,0:T(8,128)(2,1)} %get-tuple-element.5) | copy-start | bytes 4718596

commit v4 on v3

--- a/solution.py
+++ b/solution.py
@@ -30,8 +30,9 @@
     updated_h, fresh_h,
     x_v, mod_v, w_v, wo_v, gains_v, text_v, keep_v, stale_v,
     normed, message, arrived, extra, raw, q_own, kbuf, vbuf, mbuf, acc, attended, y_sum, y_out, y_in, fresh_v, updated_v, order_s, count_s,
+    mask_b, kst, vst, r_out, r_in, t_out, t_in,
     load_sem, part_send, part_recv, p1_send, p1_recv, f_send, f_recv, e_send, e_recv, y_send, y_recv, out_sem,
-    left_ready, partner_ready,
+    r_send, r_recv, t_send, t_recv, left_ready, partner_ready,
 ):
     rows, width = x_v.shape
     patch, local = stale_v.shape[1], stale_v.shape[2]
@@ -40,6 +41,8 @@
     heads = local // hd
     half_heads = heads // 2
     half = half_heads * hd
+    back = half_heads - 1
+    back_cols = slice(back * hd, (back + 1) * hd)
     sub = rows // CHUNKS
     wide = 2 * hd
     sections = lax.axis_size("section")
@@ -126,7 +129,27 @@
             device_id_type=MESH,
         )
 
-    extras = [(kind, i) for i in range(half_heads) for kind in range(2)]
+    def r_copy(n, c, side):
+        return pltpu.make_async_remote_copy(
+            src_ref=r_out.at[n, c],
+            dst_ref=r_in.at[side, c],
+            send_sem=r_send.at[n, c],
+            recv_sem=r_recv.at[side, c],
+            device_id=nbr_of[n],
+            device_id_type=MESH,
+        )
+
+    def t_copy(n, c, side):
+        return pltpu.make_async_remote_copy(
+            src_ref=t_out.at[n, c],
+            dst_ref=t_in.at[side, c],
+            send_sem=t_send.at[n, c],
+            recv_sem=t_recv.at[side, c],
+            device_id=nbr_of[n],
+            device_id_type=MESH,
+        )
+
+    extras = [(kind, i) for i in range(back) for kind in range(2)]
 
     def send_extras(n):
         for kind, i in extras:
@@ -201,7 +224,9 @@
         low = part * hd
         mbuf[low : low + hd, :] = keep_column(place, part)
         for n in range(2):
-            mbuf[near + n * patch + low : near + n * patch + low + hd, :] = keep_column(nbr_place[n], part)
+            column = keep_column(nbr_place[n], part)
+            mbuf[near + n * patch + low : near + n * patch + low + hd, :] = column
+            mask_b[n * patch + low : n * patch + low + hd, :] = jnp.where(full(is_b[n], column.shape), column, 0.0)
     live = lax.broadcasted_iota(jnp.int32, (text_rows, hd), 0) < count_s[0]
     mbuf[patch:near, :] = jnp.where(live, 1.0, 0.0).astype(BF16)
 
@@ -238,12 +263,19 @@
             pl.when((place > 0) & jnp.logical_not(waits))(lambda: send_extras(0))
             for c in range(CHUNKS):
                 part_copy(c, 1 - h).wait_recv()
-        for index in (1, 2, 0):
-            if step == 0:
-                loads[{1: 5, 2: 6, 0: 7}[index]].wait()
-            if step == 1 and index == 1:
-                loads[8].wait()
-            own(at, index, step == 1 and index == 1)
+        if step == 0:
+            loads[5].wait()
+            loads[6].wait()
+        else:
+            loads[8].wait()
+        own(at, 1, step == 1)
+        own(at, 2, False)
+        if step == 0:
+            loads[7].wait()
+        else:
+            kst[...] = head_norm(stale_v[0, :, back_cols].astype(F32), k_gain).astype(BF16)
+            vst[...] = stale_v[1, :, back_cols] * mbuf[:patch, :]
+        own(at, 0, False)
         pltpu.make_async_copy(fresh_v.at[:, at, :], fresh_h.at[:, at, :], out_sem.at[step]).start()
 
     def take(n, c):
@@ -259,14 +291,21 @@
         return matmul(weight, jnp.concatenate([vbuf[at, cols], mbuf[at, :]], axis=1))
 
     pl.when(place == 0)(lambda: take(1, 0))
-    for i in range(heads):
+    for i in range(half_heads):
         acc[i] = attend(slice(0, near), i)
+
+    def own_rest():
+        for i in range(half_heads, heads):
+            acc[i] = attend(slice(0, near), i)
+
+    pl.when(place > 0)(own_rest)
 
     def job(n, c):
         forward_copy(n, c, 1 - h).wait_recv()
         tokens = arrived.at[c, pl.ds(2 * n * sub, 2 * sub), :]
         pick = full(is_b[n], (sub, hd))
-        for i in reversed(range(local // wide)):
+
+        def project(i):
             block = slice(i * wide, (i + 1) * wide)
             for kind in range(2):
                 result = matmul(tokens[...], w_v[1 + kind, :, block]).astype(BF16)
@@ -276,6 +315,13 @@
                     for core in range(2):
                         part = result[core * sub : (core + 1) * sub, j * hd : (j + 1) * hd]
                         row = pl.multiple_of(core * rows + c * sub, sub)
+                        if head == back:
+                            to = pl.ds(pl.multiple_of(near + n * patch + row, sub), sub)
+                            if kind == 0:
+                                kbuf[to, cols] = head_norm(part.astype(F32), k_gain).astype(BF16)
+                            else:
+                                vbuf[to, cols] = part * mask_b[pl.ds(pl.multiple_of(n * patch + row, sub), sub), :]
+                            continue
                         if head < half_heads:
                             raw[n, kind, pl.ds(row, sub), cols] = part
                             continue
@@ -286,6 +332,21 @@
                             kbuf[to, cols] = head_norm(part.astype(F32), k_gain).astype(BF16)
                         else:
                             vbuf[to, cols] = part * mbuf[to, :]
+        blocks = local // wide
+        query = matmul(tokens[...], w_v[0, :, back_cols])
+        project(blocks - 1)
+        query = head_norm(query, q_gain).astype(BF16)
+        score = scores(query, kst[...])
+        for i in range(1, blocks - 1):
+            project(i)
+        weight = jnp.exp2(score).astype(BF16)
+        both = matmul(weight, jnp.concatenate([vst[...], mbuf[:patch, :]], axis=1))
+        project(0)
+        r_out[n, c] = both[:, :hd].astype(BF16)
+        for p in range(2 * sub // hd):
+            t_out[n, c, 0:1, p * hd : (p + 1) * hd] = jnp.transpose(both[p * hd : (p + 1) * hd, hd:])[0:1, :]
+        r_copy(n, c, 1 - n).start()
+        t_copy(n, c, 1 - n).start()
 
     def jobs(t, carry):
         delay = jnp.where(place == 1, CHUNKS, 0)
@@ -300,12 +361,14 @@
         pl.when(has_right & (place > 0))(lambda: take(1, t))
         pl.when(has_left)(lambda: take(0, t - delay))
 
+        pl.when(has_right)(lambda: job(1, t))
+
         @pl.when((place == 0) & (t == 0))
         def _():
             for c in range(1, CHUNKS):
                 take(1, c)
-
-        pl.when(has_right)(lambda: job(1, t))
+            own_rest()
+
         pl.when(has_left)(lambda: job(0, t - delay))
         return carry
 
@@ -327,6 +390,33 @@
             at = pl.ds(pl.multiple_of(near + jnp.where(place > 0, 0, patch), 2 * sub), patch)
             for i in which:
                 finish_head(at, i)
+
+    def back_head(at, b_at):
+        weight = jnp.exp2(scores(q_own[:, back_cols], kbuf[at, back_cols])).astype(BF16)
+        acc[back] += matmul(weight, jnp.concatenate([vbuf[at, back_cols], mask_b[b_at, :]], axis=1))
+
+    def start_back():
+        @pl.when(inner)
+        def _():
+            back_head(slice(near, near + 2 * patch), slice(0, 2 * patch))
+
+        @pl.when(jnp.logical_not(inner))
+        def _():
+            only = jnp.where(place > 0, 0, patch)
+            at = pl.ds(pl.multiple_of(near + only, 2 * sub), patch)
+            back_head(at, pl.ds(pl.multiple_of(only, patch), patch))
+
+    def add_back(n):
+        for c in range(CHUNKS):
+            r_copy(n, c, n).wait_recv()
+            t_copy(n, c, n).wait_recv()
+            for core in range(2):
+                spot = pl.ds(core * rows + c * sub, sub)
+                part = slice(core * sub, (core + 1) * sub)
+                total = jnp.transpose(jnp.broadcast_to(t_in[n, c, 0:1, part], (hd, sub)))
+                pick = full(is_a[n], total.shape)
+                acc[back, spot, :hd] += jnp.where(pick, r_in[n, c, part, :].astype(F32), 0.0)
+                acc[back, spot, hd:] += jnp.where(pick, total, 0.0)
 
     def take_extra(n, i):
         for kind in range(2):
@@ -355,17 +445,20 @@
             y_sum[:, cols] = part if first else y_sum[:, cols] + part
 
     finish_heads(range(half_heads, heads))
+    start_back()
     loads[9].wait()
     last = (half_heads - 1) // 2
     late_pairs = [pair for pair in range(heads // 2) if 2 * pair + 1 < half_heads]
     early_pairs = [pair for pair in range(heads // 2) if 2 * pair >= half_heads]
     for k, pair in enumerate(early_pairs):
         partial_sum(pair, k == 0)
-    for i in range(half_heads - 1):
+    for i in range(back):
         extra_head(i)
     for pair in late_pairs:
         partial_sum(pair, False)
-    extra_head(half_heads - 1)
+    for n in (1, 0):
+        for_neighbour(n, lambda n=n: add_back(n))
+    attended[:, back_cols] = (acc[back, :, :hd] / acc[back, :, hd:]).astype(BF16)
 
     lanes = slice(last * wide, (last + 1) * wide)
     other = pl.ds(pl.multiple_of((1 - h) * rows, rows), rows)
@@ -400,6 +493,8 @@
         for c in range(CHUNKS):
             p1_copy(n, c, 1 - n).wait_send()
             forward_copy(n, c, h).wait_send()
+            r_copy(n, c, 1 - n).wait_send()
+            t_copy(n, c, 1 - n).wait_send()
         for kind, i in extras:
             extra_copy(n, kind, i, 1 - n).wait_send()
 
@@ -468,6 +563,13 @@
             vmem((rows, width), BF16),
             pltpu.SMEM(patch_order.shape, jnp.int32),
             pltpu.SMEM(text_count.shape, jnp.int32),
+            vmem((2 * patch, hd), BF16),
+            vmem((patch, hd), BF16),
+            vmem((patch, hd), BF16),
+            vmem((2, CHUNKS, 2 * sub, hd), BF16),
+            vmem((2, CHUNKS, 2 * sub, hd), BF16),
+            vmem((2, CHUNKS, 8, 2 * sub), F32),
+            vmem((2, CHUNKS, 8, 2 * sub), F32),
             dma((11 + 2 * CHUNKS,)),
             dma((CHUNKS,)),
             dma((CHUNKS,)),
@@ -480,6 +582,10 @@
             dma((y_steps,)),
             dma((y_steps,)),
             dma((2 + y_steps,)),
+            dma((2, CHUNKS)),
+            dma((2, CHUNKS)),
+            dma((2, CHUNKS)),
+            dma((2, CHUNKS)),
             pltpu.SemaphoreType.REGULAR,
             pltpu.SemaphoreType.REGULAR,
         ],

time: 52.2 us -> 51.2 us (0.981)
  the two profiles are of different devices: /device:TPU:703 before, /device:TPU:513 now
where the time goes in v4:
time: 51.2 us; the launch traced here: 51.1 us
  Pallas kernels  46.5 us (91%)
  local copies, waits for them, and re-layouts  3.33 us (7%)
  between operations  1.3 us (3%)
    pallas_call x1, Pallas kernels, on_device(): pl.pallas_call(kernel, out_shape=(jax.ShapeDtypeStruct((rows, width), BF1...  46.5 us
    unnamed x4, local copies, waits for them, and re-layouts  3.33 us

profile of v4, /device:TPU:513, one launch (start us, length us, event | category | flops | bytes accessed | tf_op | source)
XLA Modules:
  0.0 51.1 jit_solution(8926645955536332794)
XLA Ops:
  1.3 46.5 %patch_attention.1 = (bf16[256,1536]{1,0:T(8,128)(2,1)}, bf16[2,512,768]{2,1,0:T(8,128)(2,1)}) custom-call(s32[64]{0:T(128)} %order_h.1, s32[1]{0:T(128)S(6)} %copy.14.count_h, bf16[256,1536]{1,0:T(8,128)(2,1)} %x_h.1, f32[3,1536]{1,0:T(4,128)} %mod_h.1, bf16[3,1536,768]{2,1,0:T(8,128)(2,1)} %w_h.1, bf16[768,1536]{1,0:T(8,128)(2,1)} %wo_h.1, ...), custom_call_target="tpu_custom_call" | custom-call | tf_op jit(solution)/shard_map/patch_attention/pallas_call | solution.py:531
  47.8 0.0 copy-start
  47.8 2.2 %copy.15 = bf16[256,1536]{1,0:T(8,128)(2,1)} copy(bf16[256,1536]{1,0:T(8,128)(2,1)} %get-tuple-element.4) | data formatting | bytes 1572864
  49.9 0.0 copy-done
  50.0 1.1 %copy.16 = bf16[2,512,768]{2,1,0:T(8,128)(2,1)} copy(bf16[2,512,768]{2,1,0:T(8,128)(2,1)S(1)} %copy-done) | data formatting | bytes 3145728
Async XLA Ops:
  47.8 2.2 %copy-start = (bf16[2,512,768]{2,1,0:T(8,128)(2,1)S(1)}, bf16[2,512,768]{2,1,0:T(8,128)(2,1)}, u32[]{:S(2)}) copy-start(bf16[2,512,768]{2,1,0:T(8,128)(2,1)} %get-tuple-element.5) | copy-start | bytes 4718596

commit v5 on v4

--- a/solution.py
+++ b/solution.py
@@ -177,6 +177,8 @@
         pl.semaphore_wait(partner_ready, 1)
         swap_parts()
 
+    pl.when(place == 0)(meet_right)
+
     loads[1].wait()
     loads[0].wait()
     own_slot = order_s[place]
@@ -196,7 +198,7 @@
             tokens = (shifted * lax.rsqrt(spread + epsilon) * scale + shift).astype(BF16)
             normed[pl.ds(pl.multiple_of(base + c * sub + p * piece, piece), piece), :] = tokens
             if c == 0 and p == 0:
-                meet_right()
+                pl.when(place > 0)(meet_right)
                 loads[2].wait()
             other = slice(rows + c * sub + p * piece, rows + c * sub + (p + 1) * piece)
             packed = jnp.concatenate(

time: 51.2 us -> 50.3 us (0.982); the launches traced: 51.1 us -> 49.7 us
  Pallas kernels: 46.5 us -> 45 us
    pallas_call x1, Pallas kernels: 46.5 us -> 45 us  [on_device(): pl.pallas_call(kernel, out_shape=(jax.ShapeDtypeStruct((rows, width), BF1...]
where the time goes in v5:
time: 50.3 us; the launch traced here: 49.7 us
  Pallas kernels  45 us (89%)
  local copies, waits for them, and re-layouts  3.33 us (7%)
  between operations  1.3 us (3%)
    pallas_call x1, Pallas kernels, on_device(): pl.pallas_call(kernel, out_shape=(jax.ShapeDtypeStruct((rows, width), BF1...  45 us
    unnamed x4, local copies, waits for them, and re-layouts  3.33 us

profile of v5, /device:TPU:513, one launch (start us, length us, event | category | flops | bytes accessed | tf_op | source)
XLA Modules:
  0.0 49.7 jit_solution(14243716656051722112)
XLA Ops:
  1.3 45.0 %patch_attention.1 = (bf16[256,1536]{1,0:T(8,128)(2,1)}, bf16[2,512,768]{2,1,0:T(8,128)(2,1)}) custom-call(s32[64]{0:T(128)} %order_h.1, s32[1]{0:T(128)S(6)} %copy.14.count_h, bf16[256,1536]{1,0:T(8,128)(2,1)} %x_h.1, f32[3,1536]{1,0:T(4,128)} %mod_h.1, bf16[3,1536,768]{2,1,0:T(8,128)(2,1)} %w_h.1, bf16[768,1536]{1,0:T(8,128)(2,1)} %wo_h.1, ...), custom_call_target="tpu_custom_call" | custom-call | tf_op jit(solution)/shard_map/patch_attention/pallas_call | solution.py:533
  46.3 0.0 copy-start
  46.3 2.2 %copy.15 = bf16[256,1536]{1,0:T(8,128)(2,1)} copy(bf16[256,1536]{1,0:T(8,128)(2,1)} %get-tuple-element.4) | data formatting | bytes 1572864
  48.5 0.0 copy-done
  48.5 1.1 %copy.16 = bf16[2,512,768]{2,1,0:T(8,128)(2,1)} copy(bf16[2,512,768]{2,1,0:T(8,128)(2,1)S(1)} %copy-done) | data formatting | bytes 3145728
Async XLA Ops:
  46.3 2.2 %copy-start = (bf16[2,512,768]{2,1,0:T(8,128)(2,1)S(1)}, bf16[2,512,768]{2,1,0:T(8,128)(2,1)}, u32[]{:S(2)}) copy-start(bf16[2,512,768]{2,1,0:T(8,128)(2,1)} %get-tuple-element.5) | copy-start | bytes 4718596
